TPU v7x, 256 devices: a whole 4x4x8 slice. The times are simulated.
256 devices in a mesh: seq: 8 (over y, x_lo), exp: 32 (over z, x_hi, core).
Axes of the slice: x: 4 (x_hi: 2, x_lo: 2; x = x_hi * 2 + x_lo), y: 4, z: 8, core: 2. Of those that a mesh axis runs over, the one named last changes fastest.
Arguments:
- tokens: bfloat16 [65536, 2048], P(('seq', 'exp')), may hold values from -128 to 128
- slot_embed: bfloat16 [2048, 256], P(None, 'exp'), may hold values from -0.397747564 to 0.397747564
- expert_in: bfloat16 [64, 2048, 4096], P('exp', None, 'seq'), may hold values from -0.125 to 0.125
- expert_out: bfloat16 [64, 4096, 2048], P('exp', 'seq'), may hold values from -0.09375 to 0.09375
- out_grad: bfloat16 [65536, 2048], P(('seq', 'exp')), may hold values from -0.59765625 to 0.59765625
Outputs:
- tok_grad: bfloat16 [65536, 2048], P(('seq', 'exp'))
- slot_grad: float32 [2048, 256], P('seq', 'exp')
All inputs are finite; a program needn't handle non-finite values.
Results may differ from a plain program's by a relative error of at most 0.024.
Values may be sent and summed in bfloat16 or wider, within the bound.
A program may use at most 64 MiB of HBM per device.

v0:
```python
from functools import partial
import functools

import jax
import jax.numpy as jnp
from jax import lax
from jax.sharding import Mesh
from jax.sharding import PartitionSpec as P

EXP = ("exp_0", "exp_1", "exp_2")
SEQ = ("seq_0", "seq_1")
SEQ_EXP = ("seq_0", "seq_1", "exp_0", "exp_1", "exp_2")


def split_up(x, dim, size):
    shape = x.shape
    blocks = x.reshape(*shape[:dim], size, shape[dim] // size, *shape[dim + 1 :])
    return jnp.moveaxis(blocks, dim, 0)


def sum_at_owner(x, axis, dim):
    size = lax.axis_size(axis)
    blocks = lax.all_to_all(split_up(x, dim, size), axis, 0, 0, tiled=True)
    return jnp.sum(blocks, axis=0)


def from_everyone(x, axis):
    copies = jnp.broadcast_to(x, (lax.axis_size(axis), *x.shape))
    return lax.all_to_all(copies, axis, split_axis=0, concat_axis=0, tiled=True)


def taken_together(x, axis):
    return from_everyone(x, axis).sum(axis=0)


def collected_together(x, axis):
    leaves = jax.tree.leaves(x)
    turns = sorted(range(len(leaves)), key=lambda k: -leaves[k].size)
    width = (1, *leaves[turns[0]].shape)[-1]
    lines = [
        jnp.pad(leaves[k].reshape(-1), (0, -leaves[k].size % width)).reshape(-1, width)
        for k in turns
    ]
    both, at, found = (lax.all_gather(jnp.concatenate(lines), axis), 0, {})
    for k, line in zip(turns, lines):
        section = both[:, at : at + len(line)].reshape(len(both), -1)
        found[k] = section[:, : leaves[k].size].reshape(-1, *leaves[k].shape)
        at += len(line)
    numbers = iter(range(len(leaves)))
    return jax.tree.map(lambda _: found[next(numbers)], x)


def joined_all(x, axes, combine):
    for axis in axes:
        pieces = collected_together(x, axis)
        x = jax.tree.map(lambda part: part[0], pieces)
        for k in range(1, lax.axis_size(axis)):
            x = combine(x, jax.tree.map(lambda part: part[k], pieces))
    return x


def one_axis_at_a_time(x, axes):
    return functools.reduce(lax.psum, axes, x)


def contract_rows(left, right):
    return lax.dot_general(
        left, right, (((0,), (0,)), ((), ())), preferred_element_type=jnp.float32
    )


def contract_cols(left, right):
    return lax.dot_general(
        left, right, (((1,), (1,)), ((), ())), preferred_element_type=jnp.float32
    )


def merge_stats(first_pair, second_pair):
    top_value = jnp.maximum(first_pair[0], second_pair[0])
    summed = first_pair[1] * jnp.exp(first_pair[0] - top_value) + second_pair[1] * jnp.exp(
        second_pair[0] - top_value
    )
    return (top_value, summed)


def owner_sum(partial_rows):
    owned = sum_at_owner(partial_rows, EXP, 0)
    return taken_together(owned, SEQ)


def shards(tokens, slot_embed, expert_in, expert_out, out_grad):
    experts_here = expert_in.shape[0]
    model_width = tokens.shape[1]
    slot_table = lax.all_gather(slot_embed, EXP, axis=1, tiled=True)
    logits = jnp.dot(tokens, slot_table, preferred_element_type=jnp.float32)
    local_top = jnp.max(logits, axis=0)
    local_total = jnp.sum(jnp.exp(logits - local_top), axis=0)
    col_top, col_total = joined_all((local_top, local_total), SEQ_EXP, merge_stats)
    dispatch = jnp.exp(logits - col_top) / col_total
    dispatch_b = dispatch.astype(jnp.bfloat16)
    combine_w = jax.nn.softmax(logits, axis=1)
    combine_b = combine_w.astype(jnp.bfloat16)
    slot_sum = owner_sum(contract_rows(dispatch_b, tokens))
    slot_in = slot_sum.astype(jnp.bfloat16).reshape(experts_here, -1, model_width)
    pre_act = jnp.einsum("esd,edh->esh", slot_in, expert_in, preferred_element_type=jnp.float32)
    hidden = jax.nn.gelu(pre_act, approximate=True).astype(jnp.bfloat16)
    out_part = jnp.einsum("esh,ehd->esd", hidden, expert_out, preferred_element_type=jnp.float32)
    slot_out = taken_together(out_part, SEQ).astype(jnp.bfloat16).reshape(-1, model_width)
    slot_all = lax.all_gather(slot_out, EXP, axis=0, tiled=True)
    comb_grad = contract_cols(out_grad, slot_all)
    grad_out = owner_sum(contract_rows(combine_b, out_grad))
    grad_out = grad_out.astype(jnp.bfloat16).reshape(experts_here, -1, model_width)
    hid_grad = jnp.einsum("esd,ehd->esh", grad_out, expert_out, preferred_element_type=jnp.float32)
    _, pullback = jax.vjp(partial(jax.nn.gelu, approximate=True), pre_act)
    act_grad = pullback(hid_grad)[0].astype(jnp.bfloat16)
    in_part = jnp.einsum("esh,edh->esd", act_grad, expert_in, preferred_element_type=jnp.float32)
    grad_own = taken_together(in_part, SEQ).astype(jnp.bfloat16).reshape(-1, model_width)
    grad_all = lax.all_gather(grad_own, EXP, axis=0, tiled=True)
    disp_grad = contract_cols(tokens, grad_all)
    centre_local = jnp.sum(dispatch_b.astype(jnp.float32) * disp_grad, axis=0)
    centre = one_axis_at_a_time(centre_local, SEQ_EXP)
    comb_mean = jnp.sum(combine_w * comb_grad, axis=1, keepdims=True)
    logit_grad = dispatch * (disp_grad - centre) + combine_w * (comb_grad - comb_mean)
    logit_b = logit_grad.astype(jnp.bfloat16)
    tok_grad = jnp.dot(dispatch_b, grad_all, preferred_element_type=jnp.float32) + contract_cols(
        logit_b, slot_table
    )
    table_part = contract_rows(tokens, logit_b)
    table_owned = sum_at_owner(table_part, EXP, 1)
    slot_grad = sum_at_owner(table_owned, SEQ, 0)
    return (tok_grad.astype(jnp.bfloat16), slot_grad)


def solution(mesh):
    torus = Mesh(mesh.devices.reshape(4, 2, 8, 2, 2), ("seq_0", "seq_1", "exp_0", "exp_1", "exp_2"))
    placed = (
        P(SEQ_EXP, None),
        P(None, EXP),
        P(EXP, None, SEQ),
        P(EXP, SEQ, None),
        P(SEQ_EXP, None),
    )
    return jax.shard_map(
        shards,
        mesh=torus,
        in_specs=placed,
        out_specs=(P(SEQ_EXP, None), P(SEQ, EXP)),
        check_vma=False,
    )
```

profile of v0, /device:TPU:1, one launch (start us, length us, event | category | flops | bytes accessed | tf_op | source)
XLA Modules:
  0.0 531.8 jit_solution(1406648568173986912)
XLA Ops:
  7.9 84.8 %all-gather.14.cloned.1.call-done = bf16[2048,256]{0,1:T(8,128)(2,1)} async-done(((bf16[2048,8]{0,1:T(8,128)(2,1)}), bf16[2048,256]{0,1:T(8,128)(2,1)}) %all-gather.14.cloned.1.call-update) | async-done | bytes 1048592 | tf_op jit(solution)/shard_map/all_gather | solution.py:94
  94.7 8.5 %all-gather.5 = f32[4,2,256]{2,1,0:T(2,128)S(1)} all-gather(f32[1,2,256]{2,1,0:T(2,128)S(1)} %maximum_bitcast_fusion), channel_id=2, replica_groups=mesh['seq_0'=4,'seq_1'=2,'exp_0'=8,'exp_1'=2,'exp_2'=2] {'seq_0'}, dimensions={0}, use_global_device_ids=true | all-gather | bytes 10240 | tf_op jit(solution)/shard_map/all_gather | solution.py:44
  103.2 3.2 all-gather.6
  106.4 15.6 %all-gather.7 = f32[8,2,256]{2,1,0:T(2,128)S(1)} all-gather(f32[1,2,256]{2,1,0:T(2,128)S(1)} %maximum_bitcast_fusion.2), channel_id=4, replica_groups=mesh['seq_0'=4,'seq_1'=2,'exp_0'=8,'exp_1'=2,'exp_2'=2] {'exp_0'}, dimensions={0}, use_global_device_ids=true | all-gather | bytes 18432 | tf_op jit(solution)/shard_map/all_gather | solution.py:44
  122.1 4.7 all-gather.8
  126.9 12.8 %all-gather.9 = f32[2,2,256]{2,1,0:T(2,128)S(1)} all-gather(f32[1,2,256]{2,1,0:T(2,128)S(1)} %maximum_bitcast_fusion.4), channel_id=6, replica_groups=mesh['seq_0'=4,'seq_1'=2,'exp_0'=8,'exp_1'=2,'exp_2'=2] {'exp_2'}, dimensions={0}, use_global_device_ids=true | all-gather | bytes 6144 | tf_op jit(solution)/shard_map/all_gather | solution.py:44
  141.4 5.1 all-to-all-start.2
  146.6 3.2 convolution_bitcast_fusion.2
  149.7 46.9 %all-to-all-done.2 = f32[32,8,2048]{2,1,0:T(8,128)S(1)} async-done(((f32[32,8,2048]{2,1,0:T(8,128)}), f32[32,8,2048]{2,1,0:T(8,128)S(1)}, u32[]{:S(2)}, u32[]{:S(2)}) %all-to-all-start.2) | async-done | bytes 2097184 | tf_op jit(solution)/shard_map/all_to_all | solution.py:23
  197.9 6.4 %all-to-all-start = ((f32[32,8,2048]{2,1,0:T(8,128)}), f32[32,8,2048]{2,1,0:T(8,128)S(1)}, u32[]{:S(2)}, u32[]{:S(2)}) async-start(f32[32,8,2048]{2,1,0:T(8,128)} %convolution_bitcast_fusion.2), calls=%async_computation | async-start | bytes 4194304 | tf_op jit(solution)/shard_map/all_to_all | solution.py:23
  206.0 48.4 %all-to-all-done = f32[32,8,2048]{2,1,0:T(8,128)S(1)} async-done(((f32[32,8,2048]{2,1,0:T(8,128)}), f32[32,8,2048]{2,1,0:T(8,128)S(1)}, u32[]{:S(2)}, u32[]{:S(2)}) %all-to-all-start) | async-done | bytes 2097184 | tf_op jit(solution)/shard_map/all_to_all | solution.py:23
  255.2 4.1 all-to-all-start.3
  259.5 9.3 %all-to-all-done.3 = f32[8,8,2048]{2,1,0:T(8,128)} async-done(((f32[8,8,2048]{2,1,0:T(8,128)}), f32[8,8,2048]{2,1,0:T(8,128)}, u32[]{:S(2)}, u32[]{:S(2)}) %all-to-all-start.3) | async-done | bytes 524320 | tf_op jit(solution)/shard_map/all_to_all | solution.py:29
  269.6 3.5 all-to-all-start.1
  274.2 7.3 %all-to-all-done.1 = f32[8,8,2048]{2,1,0:T(8,128)S(1)} async-done(((f32[8,8,2048]{2,1,0:T(8,128)}), f32[8,8,2048]{2,1,0:T(8,128)S(1)}, u32[]{:S(2)}, u32[]{:S(2)}) %all-to-all-start.1) | async-done | bytes 524320 | tf_op jit(solution)/shard_map/all_to_all | solution.py:29
  281.6 2.8 fusion.96
  284.4 5.7 %fusion.12 = f32[2,4,2048]{2,1,0:T(4,128)S(1)} fusion(bf16[2,2048,512]{2,1,0:T(8,128)(2,1)} %param.7, f32[2,4,512]{2,1,0:T(4,128)S(1)} %fusion.96, bf16[2,4,2048]{2,1,0:T(4,128)(2,1)S(1)} %convert_element_type.52, bf16[2,512,2048]{2,1,0:T(8,128)(2,1)} %param.8), kind=kOutput, calls=%fused_computation.27 | convolution fusion | flops 33636352 | bytes 8503296 | tf_op jit(solution)/shard_map/esh,edh->esd/dot_general | solution.py:116
  290.3 10.9 %all_to_all.40 = f32[8,2,4,2048]{3,2,1,0:T(4,128)S(1)} all-to-all(f32[8,2,4,2048]{3,2,1,0:T(4,128)S(1)} %broadcast_in_dim.10), channel_id=1, replica_groups=mesh['seq_0'=4,'seq_1'=2,'exp_0'=8,'exp_1'=2,'exp_2'=2] {'seq_0','seq_1'}, dimensions={0} | all-to-all | bytes 1048576 | tf_op jit(solution)/shard_map/all_to_all | solution.py:29
  302.0 2.9 fusion.14
  305.0 10.2 %all_to_all.41 = f32[8,2,4,2048]{3,2,1,0:T(4,128)S(1)} all-to-all(f32[8,2,4,2048]{3,2,1,0:T(4,128)S(1)} %broadcast_in_dim.22), channel_id=1, replica_groups=mesh['seq_0'=4,'seq_1'=2,'exp_0'=8,'exp_1'=2,'exp_2'=2] {'seq_0','seq_1'}, dimensions={0} | all-to-all | bytes 1048576 | tf_op jit(solution)/shard_map/all_to_all | solution.py:29
  315.9 61.8 %all-gather.16.cloned.1.call-done = bf16[256,2048]{1,0:T(8,128)(2,1)} async-done(((bf16[8,2048]{1,0:T(8,128)(2,1)}), bf16[256,2048]{1,0:T(8,128)(2,1)}) %all-gather.16.cloned.1.call-update) | async-done | bytes 1048592 | tf_op jit(solution)/shard_map/all_gather | solution.py:118
  379.5 8.5 %psum.35 = f32[256]{0:T(256)S(1)} all-reduce(f32[256]{0:T(256)S(1)} %get-tuple-element.23), channel_id=1, replica_groups=mesh['seq_0'=4,'seq_1'=2,'exp_0'=8,'exp_1'=2,'exp_2'=2] {'seq_0'}, use_global_device_ids=true, to_apply=%region_10.11 | all-reduce | flops 256 | bytes 2048 | tf_op jit(solution)/shard_map/psum | solution.py:63
  388.0 3.8 psum.36
  391.7 12.3 %psum.37 = f32[256]{0:T(256)S(1)} all-reduce(f32[256]{0:T(256)S(1)} %psum.36), channel_id=1, replica_groups=mesh['seq_0'=4,'seq_1'=2,'exp_0'=8,'exp_1'=2,'exp_2'=2] {'exp_0'}, use_global_device_ids=true, to_apply=%region_12.13 | all-reduce | flops 256 | bytes 2048 | tf_op jit(solution)/shard_map/psum | solution.py:63
  404.0 5.3 psum.38
  409.2 10.5 %psum.39 = f32[256]{0:T(256)S(1)} all-reduce(f32[256]{0:T(256)S(1)} %psum.38), channel_id=1, replica_groups=mesh['seq_0'=4,'seq_1'=2,'exp_0'=8,'exp_1'=2,'exp_2'=2] {'exp_2'}, use_global_device_ids=true, to_apply=%region_14.15 | all-reduce | flops 256 | bytes 2048 | tf_op jit(solution)/shard_map/psum | solution.py:63
  419.7 35.5 %all-gather.18.cloned.1.call-done = bf16[256,2048]{1,0:T(8,128)(2,1)} async-done(((bf16[8,2048]{1,0:T(8,128)(2,1)}), bf16[256,2048]{1,0:T(8,128)(2,1)}) %all-gather.18.cloned.1.call-update) | async-done | bytes 1048592 | tf_op jit(solution)/shard_map/all_gather | solution.py:109
  459.0 5.6 %all-to-all-start.6 = ((f32[32,2048,8]{1,2,0:T(8,128)}), f32[32,2048,8]{1,2,0:T(8,128)S(1)}, u32[]{:S(2)}, u32[]{:S(2)}) async-start(f32[32,2048,8]{1,2,0:T(8,128)} %convolution_bitcast_fusion), calls=%async_computation.6 | async-start | bytes 4194304 | tf_op jit(solution)/shard_map/all_to_all | solution.py:23
  464.6 3.0 fusion.93
  467.6 47.0 %all-to-all-done.6 = f32[32,2048,8]{1,2,0:T(8,128)S(1)} async-done(((f32[32,2048,8]{1,2,0:T(8,128)}), f32[32,2048,8]{1,2,0:T(8,128)S(1)}, u32[]{:S(2)}, u32[]{:S(2)}) %all-to-all-start.6) | async-done | bytes 2097184 | tf_op jit(solution)/shard_map/all_to_all | solution.py:23
  515.4 4.0 all-to-all-start.7
  519.4 3.6 fusion
  (50 shorter events, 20.7 us)
Async XLA Ops:
  7.2 85.5 %copy-start = (bf16[256,2048]{1,0:T(8,128)(2,1)S(1)}, bf16[256,2048]{1,0:T(8,128)(2,1)}, u32[]{:S(2)}) copy-start(bf16[256,2048]{1,0:T(8,128)(2,1)} %param.5) | copy-start | bytes 3145732
  7.2 85.5 %all-gather.14.cloned.1.call-start = ((), (), s32[]{:S(2)}) async-start(), calls=%async_computation.8 | async-start | bytes 1081344 | tf_op jit(solution)/shard_map/all_gather | solution.py:94
  141.4 55.2 %all-to-all-start.2 = ((f32[32,8,2048]{2,1,0:T(8,128)}), f32[32,8,2048]{2,1,0:T(8,128)S(1)}, u32[]{:S(2)}, u32[]{:S(2)}) async-start(f32[32,8,2048]{2,1,0:T(8,128)} %convolution_bitcast_fusion.1), calls=%async_computation.2 | async-start | bytes 4194304 | tf_op jit(solution)/shard_map/all_to_all | solution.py:23
  196.6 1.3 copy-start.1
  197.9 56.4 %all-to-all-start = ((f32[32,8,2048]{2,1,0:T(8,128)}), f32[32,8,2048]{2,1,0:T(8,128)S(1)}, u32[]{:S(2)}, u32[]{:S(2)}) async-start(f32[32,8,2048]{2,1,0:T(8,128)} %convolution_bitcast_fusion.2), calls=%async_computation | async-start | bytes 4194304 | tf_op jit(solution)/shard_map/all_to_all | solution.py:23
  255.2 13.5 %all-to-all-start.3 = ((f32[8,8,2048]{2,1,0:T(8,128)}), f32[8,8,2048]{2,1,0:T(8,128)}, u32[]{:S(2)}, u32[]{:S(2)}) async-start(f32[8,8,2048]{2,1,0:T(8,128)} %broadcast_in_dim.9), calls=%async_computation.3 | async-start | bytes 1048576 | tf_op jit(solution)/shard_map/all_to_all | solution.py:29
  269.6 12.0 %all-to-all-start.1 = ((f32[8,8,2048]{2,1,0:T(8,128)}), f32[8,8,2048]{2,1,0:T(8,128)S(1)}, u32[]{:S(2)}, u32[]{:S(2)}) async-start(f32[8,8,2048]{2,1,0:T(8,128)} %broadcast_in_dim.8), calls=%async_computation.1 | async-start | bytes 1048576 | tf_op jit(solution)/shard_map/all_to_all | solution.py:29
  273.1 104.7 %all-gather.16.cloned.1.call-start = ((), (), s32[]{:S(2)}) async-start(), calls=%async_computation.9 | async-start | bytes 1081344 | tf_op jit(solution)/shard_map/all_gather | solution.py:118
  301.9 153.3 %copy-start.2 = (bf16[256,2048]{1,0:T(8,128)(2,1)S(1)}, bf16[256,2048]{1,0:T(8,128)(2,1)}, u32[]{:S(2)}) copy-start(bf16[256,2048]{1,0:T(8,128)(2,1)} %param.9) | copy-start | bytes 3145732
  302.0 153.3 %all-gather.18.cloned.1.call-start = ((), (), s32[]{:S(2)}) async-start(), calls=%async_computation.10 | async-start | bytes 1081344 | tf_op jit(solution)/shard_map/all_gather | solution.py:109
  379.5 79.5 %copy-start.3 = (f32[256,256]{1,0:T(8,128)}, f32[256,256]{1,0:T(8,128)S(1)}, u32[]{:S(2)}) copy-start(f32[256,256]{1,0:T(8,128)S(1)} %get-tuple-element.24) | copy-start | bytes 786436
  457.1 1.9 copy-start.4
  459.0 55.6 %all-to-all-start.6 = ((f32[32,2048,8]{1,2,0:T(8,128)}), f32[32,2048,8]{1,2,0:T(8,128)S(1)}, u32[]{:S(2)}, u32[]{:S(2)}) async-start(f32[32,2048,8]{1,2,0:T(8,128)} %convolution_bitcast_fusion), calls=%async_computation.6 | async-start | bytes 4194304 | tf_op jit(solution)/shard_map/all_to_all | solution.py:23
  515.4 9.3 %all-to-all-start.7 = ((f32[8,256,8]{1,2,0:T(8,128)}), f32[8,256,8]{1,2,0:T(8,128)S(1)}, u32[]{:S(2)}, u32[]{:S(2)}) async-start(f32[8,256,8]{1,2,0:T(8,128)} %bitcast.50), calls=%async_computation.7 | async-start | bytes 131072 | tf_op jit(solution)/shard_map/all_to_all | solution.py:23
Sparse Core Ops, SparseCore 0:
  10.8 81.8 all-gather.13
  302.1 75.6 all-gather.15
  380.6 74.6 all-gather.17
where the time goes:
time: 534 us; the launch traced here: 532 us
  waiting for transfers between devices  343 us (64%)
  blocking collectives  106 us (20%)
  matrix products  30.2 us (6%)
  starting transfers between devices  28.9 us (5%)
  between operations  13.9 us (3%)
    all_to_all x4, waiting for transfers between devices, sum_at_owner(): blocks = lax.all_to_all(split_up(x, dim, size), axis, 0, 0, tiled=True)  144 us
    all_gather x1, waiting for transfers between devices, shards(): slot_table = lax.all_gather(slot_embed, EXP, axis=1, tiled=True)  84.8 us
    all_gather x1, waiting for transfers between devices, shards(): grad_all = lax.all_gather(grad_own, EXP, axis=0, tiled=True)  61.8 us
    all_gather x5, blocking collectives, collected_together(): both, at, found = (lax.all_gather(jnp.concatenate(lines), axis), 0, {})  44.8 us
    psum x5, blocking collectives, one_axis_at_a_time(): return functools.reduce(lax.psum, axes, x)  40.3 us
    all_gather x1, waiting for transfers between devices, shards(): slot_all = lax.all_gather(slot_out, EXP, axis=0, tiled=True)  35.5 us
    all_to_all x4, starting transfers between devices, sum_at_owner(): blocks = lax.all_to_all(split_up(x, dim, size), axis, 0, 0, tiled=True)  21.1 us
    all_to_all x2, blocking collectives, from_everyone(): return lax.all_to_all(copies, axis, split_axis=0, concat_axis=0, tiled=True)  21.1 us
  transfers between devices with their start and end apart: 9, of which 9 were waited for; matrix products, arithmetic and copies ran while one was open for 3% of the time, Pallas kernels for 0%

commit v1 on v0

v1 whole, which is shorter than its diff:
```python
import functools

import jax
import jax.numpy as jnp
from jax import lax
from jax.experimental import pallas as pl
from jax.experimental.pallas import tpu as pltpu
from jax.sharding import Mesh
from jax.sharding import PartitionSpec as P

EXP = ("exp_0", "exp_1", "exp_2")
SEQ = ("seq_0", "seq_1")
SEQ_EXP = ("seq_0", "seq_1", "exp_0", "exp_1", "exp_2")
AXES = SEQ_EXP
F32, BF16 = jnp.float32, jnp.bfloat16
ROOT = 0.7978845608028654


def rows_dot(left, right):
    return lax.dot_general(left, right, (((1,), (0,)), ((), ())), preferred_element_type=F32)


def cols_dot(left, right):
    return lax.dot_general(left, right, (((1,), (1,)), ((), ())), preferred_element_type=F32)


def gelu_and_slope(v):
    t = jnp.tanh(ROOT * (v + 0.044715 * (v * v * v)))
    value = 0.5 * v * (1.0 + t)
    slope = 0.5 * (1.0 + t) + 0.5 * v * (1.0 - t * t) * (ROOT * (1.0 + 3.0 * 0.044715 * (v * v)))
    return value, slope


def flat(block):
    block = block.astype(F32)
    return block.reshape(-1, block.shape[-1])


def kernel(
    sizes,
    tok_hbm, slot_hbm, win_hbm, wout_hbm, og_hbm,
    tg_hbm, sg_out,
    tok, og, win, wout, tok_t, og_t, table, grads, logits, weight, comb_f, comb_g, disp_g,
    both, tg, factor,
    gath_a, gath_d,
    pb, pb1, pb2, pb3, rbc, rb1, rb2, rbz,
    pg, pg1, pg2, pg3, rgc, rg1, rg2, rgz,
    stat, stat_c, stat_1, stat_2, stat_z,
    cen, cen_z, cen_1, cen_2, cen_c,
    seq_in, seq_out, seq_rec,
    local_sem, send_sem, recv_sem,
):
    Y, XL, Z, XH, C = sizes
    N, NQ = XL * XH, Y * XL
    assert Y == N and C == 2
    S = C * XH * Z * 8
    W = tok.shape[1] // NQ
    HALF = W // 2
    ZR = Z * 8
    y, xl, z, xh, c = (lax.axis_index(name) for name in AXES)
    x, q = xh * XL + xl, y * XL + xl
    rem, div = lax.rem, lax.div

    def z_to(i):
        k = rem(z + i, Z)
        return k, {"exp_0": k}

    def y_to(i):
        k = rem(y + i, N)
        return k, {"seq_0": k}

    def x_to(i):
        k = rem(x + i, N)
        return k, {"exp_1": div(k, XL), "seq_1": rem(k, XL)}

    def q_to(i):
        k = rem(q + i, NQ)
        return k, {"seq_0": div(k, XL), "seq_1": rem(k, XL)}

    other = {"exp_2": 1 - c}
    MESH = pl.DeviceIdType.MESH
    count = [0]
    begun = []

    def send(src, dst, device):
        k = count[0]
        count[0] += 1
        copy = pltpu.make_async_remote_copy(
            src_ref=src, dst_ref=dst, send_sem=send_sem.at[k], recv_sem=recv_sem.at[k],
            device_id=device, device_id_type=MESH,
        )
        copy.start()
        begun.append(copy)
        return copy

    def arrive(copies):
        for copy in copies:
            copy.wait_recv()

    slot_copy = pltpu.make_async_copy
    first = [
        slot_copy(
            slot_hbm.at[:, pl.ds(pl.multiple_of(q * W + a * HALF, HALF), HALF)],
            gath_a.at[a, y, xl, c, xh, z],
            local_sem.at[a],
        )
        for a in range(2)
    ]
    big = [
        slot_copy(src, dst, local_sem.at[2 + k])
        for k, (src, dst) in enumerate(((tok_hbm, tok), (og_hbm, og), (win_hbm, win), (wout_hbm, wout)))
    ]
    for copy in first + big:
        copy.start()

    barrier = pltpu.get_barrier_semaphore()
    partners = [z_to(i)[1] for i in range(1, Z)]
    partners += [y_to(i)[1] for i in range(1, N)]
    partners += [x_to(i)[1] for i in range(1, N)]
    partners += [q_to(i)[1] for i in range(1, NQ)]
    partners += [other]
    for device in partners:
        pl.semaphore_signal(barrier, inc=1, device_id=device, device_id_type=MESH)
    pl.semaphore_wait(barrier, len(partners))

    def gather(buf, beside=None):
        moves = [send(buf.at[:, y, xl, c, xh, z], buf.at[:, y, xl, c, xh, z], z_to(i)[1]) for i in range(1, Z)]
        if beside:
            own, over_z, over_1, over_2, over_c = beside
            moves += [send(own.at[0], over_z.at[i - 1], z_to(i)[1]) for i in range(1, Z)]
        yield "sent"
        arrive(moves)
        moves = []
        for i in range(1, N):
            moves.append(send(buf.at[0, y, xl, c, xh], buf.at[0, y, xl, c, xh], x_to(i)[1]))
            moves.append(send(buf.at[1, y, xl, c, xh], buf.at[1, y, xl, c, xh], y_to(i)[1]))
        if beside:
            total = own[0]
            for i in range(1, Z):
                total += over_z[i - 1]
            own[1] = total
            moves += [send(own.at[1], over_1.at[i - 1], x_to(i)[1]) for i in range(1, N)]
        arrive(moves)
        moves = []
        for i in range(1, N):
            moves.append(send(buf.at[0, y, :, c], buf.at[0, y, :, c], y_to(i)[1]))
            moves.append(send(buf.at[1, :, xl, c, xh], buf.at[1, :, xl, c, xh], x_to(i)[1]))
        if beside:
            total = own[1]
            for i in range(1, N):
                total += over_1[i - 1]
            own[2] = total
            moves += [send(own.at[2], over_2.at[i - 1], y_to(i)[1]) for i in range(1, N)]
        arrive(moves)
        moves = [send(buf.at[:, :, :, c], buf.at[:, :, :, c], other)]
        if beside:
            total = own[2]
            for i in range(1, N):
                total += over_2[i - 1]
            own[3] = total
            moves += [send(own.at[3], over_c.at[0], other)]
        arrive(moves)

    lines = lax.broadcasted_iota(jnp.int32, (8, S), 0)

    def merge(entries):
        top = entries[0][0:1]
        for entry in entries[1:]:
            top = jnp.maximum(top, entry[0:1])
        scales = [jnp.exp(entry[0:1] - top) for entry in entries]
        total = entries[0][1:2] * scales[0]
        for entry, scale in zip(entries[1:], scales[1:]):
            total += entry[1:2] * scale
        turned = jnp.zeros((8, S), F32)
        for k, scale in enumerate(scales):
            turned = jnp.where(lines == k, scale, turned)
        factor[...] = jnp.concatenate([turned, jnp.zeros((120, S), F32)], axis=0).T
        return jnp.where(lines == 0, top, jnp.where(lines == 1, total, 0.0))

    def joined(parts, scaled, row, rows):
        total = None
        for k, part in enumerate(parts):
            part = flat(part)
            if scaled:
                part = part * factor[pl.ds(pl.multiple_of(row, 8), rows), k : k + 1]
            total = part if total is None else total + part
        return total

    def reduce(p, s1, s2, s3, rc, r1, r2, rz, scaled):
        w = p.shape[-1]
        moves = [send(p.at[:, 1 - c], rc, other)]
        if scaled:
            moves.append(send(stat.at[0], stat_c.at[0], other))
        yield "sent"
        arrive(moves)
        if scaled:
            stat[1] = merge([stat[0], stat_c[0]])

        def first_sum(b, _):
            for a in range(2):
                row = c * (S // 2) + div(rem(b, N), XL) * ZR
                total = joined((p[a, c, b], rc[a, b]), scaled and a == 0, row, ZR)
                s1[a, b] = total.reshape(Z, 8, w).astype(BF16)
            return 0

        lax.fori_loop(0, N * N, first_sum, 0)
        moves = []
        for i in range(1, N):
            k, device = y_to(i)
            moves.append(send(s1.at[0, pl.ds(k * N, N)], r1.at[0, i - 1], device))
            if scaled:
                moves.append(send(stat.at[1], stat_1.at[i - 1], device))
            k, device = x_to(i)
            moves.append(send(s1.at[1, pl.ds(k * N, N)], r1.at[1, i - 1], device))
        yield "sent"
        arrive(moves)
        if scaled:
            stat[2] = merge([stat[1]] + [stat_1[i] for i in range(N - 1)])

        def second_sum(b, _):
            for a, me in ((0, y), (1, x)):
                row = c * (S // 2) + div(b, XL) * ZR
                parts = [s1[a, me * N + b]] + [r1[a, i, b] for i in range(N - 1)]
                total = joined(parts, scaled and a == 0, row, ZR)
                s2[a, b] = total.reshape(Z, 8, w).astype(BF16)
            return 0

        lax.fori_loop(0, N, second_sum, 0)
        moves = []
        for i in range(1, N):
            k, device = x_to(i)
            moves.append(send(s2.at[0, k], r2.at[0, i - 1], device))
            if scaled:
                moves.append(send(stat.at[2], stat_2.at[i - 1], device))
            k, device = y_to(i)
            moves.append(send(s2.at[1, k], r2.at[1, i - 1], device))
        arrive(moves)
        if scaled:
            stat[3] = merge([stat[2]] + [stat_2[i] for i in range(N - 1)])
        for a, me in ((0, x), (1, y)):
            row = c * (S // 2) + xh * ZR
            parts = [s2[a, me]] + [r2[a, i] for i in range(N - 1)]
            total = joined(parts, scaled and a == 0, row, ZR)
            s3[a] = total.reshape(Z, 8, w).astype(BF16)
        moves = []
        for i in range(1, Z):
            k, device = z_to(i)
            moves.append(send(s3.at[:, k], rz.at[i - 1], device))
            if scaled:
                moves.append(send(stat.at[3], stat_z.at[i - 1], device))
        arrive(moves)
        if scaled:
            stat[4] = merge([stat[3]] + [stat_z[i] for i in range(Z - 1)])
        row = c * (S // 2) + xh * ZR + z * 8
        result = []
        for a in range(2):
            parts = [s3[a, z]] + [rz[i, a] for i in range(Z - 1)]
            result.append(joined(parts, scaled and a == 0, row, 8))
        yield result

    def end_of(steps):
        last = None
        for last in steps:
            pass
        return last

    own_row = pl.multiple_of(c * (S // 2) + xh * ZR + z * 8, 8)

    for copy in first:
        copy.wait()
    steps = gather(gath_a)
    next(steps)
    big[0].wait()
    tok_t[...] = tok[...].T
    big[1].wait()
    og_t[...] = og[...].T
    end_of(steps)

    def lay_table(k, _):
        for a in range(2):
            block = flat(gath_a[a, div(k, XL), rem(k, XL)]).astype(BF16)
            table[:, pl.ds(pl.multiple_of(k * W + a * HALF, HALF), HALF)] = block
        return 0

    lax.fori_loop(0, NQ, lay_table, 0)
    logits[...] = rows_dot(table[...], tok_t[...])

    lg = logits[...]
    top = jnp.max(lg, axis=1, keepdims=True)
    local = jnp.exp(lg - top)
    total = jnp.sum(local, axis=1, keepdims=True)
    lanes = lax.broadcasted_iota(jnp.int32, (S, 128), 1)
    stat[0] = jnp.where(lanes == 0, top, jnp.where(lanes == 1, total, 0.0)).T[0:8]
    raised = jnp.exp(lg - jnp.max(lg, axis=0, keepdims=True))
    comb = raised / jnp.sum(raised, axis=0, keepdims=True)
    weight[...] = comb
    local_b, comb_b = local.astype(BF16), comb.astype(BF16)

    def place(target, a, k, values):
        ky, kl = div(k, XL), rem(k, XL)
        for cc in range(C):
            for hh in range(XH):
                xx = hh * XL + kl
                at = ky * N + xx if a == 0 else xx * N + ky
                row = (cc * XH + hh) * ZR
                target[a, cc, at] = values[row : row + ZR].reshape(Z, 8, values.shape[1]).astype(BF16)

    def partial_sums(k, _):
        span = pl.ds(pl.multiple_of(k * W, W), W)
        place(pb, 0, k, rows_dot(local_b, tok[:, span]))
        place(pb, 1, k, rows_dot(comb_b, og[:, span]))
        return 0

    lax.fori_loop(0, NQ, partial_sums, 0)
    sum_chunk, grad_chunk = end_of(reduce(pb, pb1, pb2, pb3, rbc, rb1, rb2, rbz, True))

    stats = jnp.concatenate([stat[4], jnp.zeros((120, S), F32)], axis=0).T
    factor[...] = stats
    sum_chunk = sum_chunk / factor[pl.ds(own_row, 8), 1:2]
    seq_in[q, 0] = sum_chunk.astype(BF16)
    seq_in[q, 1] = grad_chunk.astype(BF16)
    moves = [send(seq_in.at[q], seq_in.at[q], q_to(i)[1]) for i in range(1, NQ)]
    big[2].wait()
    big[3].wait()
    arrive(moves)
    slot_rows = jnp.concatenate([seq_in[k, 0].astype(F32) for k in range(NQ)], axis=1)
    grad_rows = jnp.concatenate([seq_in[k, 1].astype(F32) for k in range(NQ)], axis=1)
    slot_b, grad_b = slot_rows.astype(BF16), grad_rows.astype(BF16)
    upper = lax.broadcasted_iota(jnp.int32, (8, 1), 0) < 4

    def pick(f, g):
        return jnp.where(upper, f, g)

    pre = pick(rows_dot(slot_b, win[0]), rows_dot(slot_b, win[1]))
    hidden, slope = gelu_and_slope(pre)
    hid_grad = pick(cols_dot(grad_b, wout[0]), cols_dot(grad_b, wout[1]))
    hidden = hidden.astype(BF16)
    act = (hid_grad * slope).astype(BF16)
    out_part = pick(rows_dot(hidden, wout[0]), rows_dot(hidden, wout[1]))
    in_part = pick(cols_dot(act, win[0]), cols_dot(act, win[1]))
    for k in range(NQ):
        seq_out[k, 0] = out_part[:, k * W : (k + 1) * W].astype(BF16)
        seq_out[k, 1] = in_part[:, k * W : (k + 1) * W].astype(BF16)
    moves = []
    for i in range(1, NQ):
        k, device = q_to(i)
        moves.append(send(seq_out.at[k], seq_rec.at[i - 1], device))
    arrive(moves)
    for a in range(2):
        total = seq_out[q, a].astype(F32)
        for i in range(NQ - 1):
            total += seq_rec[i, a].astype(F32)
        gath_d[a, y, xl, c, xh, z] = total.astype(BF16)
    part = jnp.sum(sum_chunk * total.astype(BF16).astype(F32), axis=1, keepdims=True)
    spots = lax.broadcasted_iota(jnp.int32, (8, S), 1)
    cen[0] = jnp.where(spots == own_row + lines, part, 0.0)
    end_of(gather(gath_d, (cen, cen_z, cen_1, cen_2, cen_c)))

    comb_g[...] = jnp.zeros_like(comb_g)
    disp_g[...] = jnp.zeros_like(disp_g)

    def back(k, _):
        span = pl.ds(pl.multiple_of(k * W, W), W)
        ky, kl = div(k, XL), rem(k, XL)
        comb_g[...] += rows_dot(flat(gath_d[0, ky, kl]).astype(BF16), og_t[span, :])
        block = flat(gath_d[1, ky, kl]).astype(BF16)
        grads[:, span] = block
        disp_g[...] += rows_dot(block, tok_t[span, :])
        return 0

    lax.fori_loop(0, NQ, back, 0)
    centre_row = jnp.sum(cen[3] + cen_c[0], axis=0, keepdims=True)
    centre = jnp.broadcast_to(centre_row, (128, S)).T[:, 0:1]
    comb = weight[...]
    comb_grad = comb_g[...]
    disp = jnp.exp(logits[...] - factor[:, 0:1]) / factor[:, 1:2]
    mean = jnp.sum(comb * comb_grad, axis=0, keepdims=True)
    logit_grad = disp * (disp_g[...] - centre) + comb * (comb_grad - mean)
    logit_b = logit_grad.astype(BF16)

    def table_sums(k, _):
        values = rows_dot(logit_b, tok[:, pl.ds(pl.multiple_of(k * W, W), W)])
        for a in range(2):
            place(pg, a, k, values[:, a * HALF : (a + 1) * HALF])
        return 0

    lax.fori_loop(0, NQ, table_sums, 0)
    steps = reduce(pg, pg1, pg2, pg3, rgc, rg1, rg2, rgz, False)
    next(steps)
    both[:, 0:S] = disp.T.astype(BF16)
    both[:, S : 2 * S] = logit_grad.T.astype(BF16)
    next(steps)

    def patch_grads(k, _):
        span = pl.ds(pl.multiple_of(k * W, W), W)
        tg[:, span] = (rows_dot(both[:, 0:S], grads[:, span]) + rows_dot(both[:, S : 2 * S], table[:, span])).astype(BF16)
        return 0

    lax.fori_loop(0, NQ, patch_grads, 0)
    out_copy = pltpu.make_async_copy(tg, tg_hbm, local_sem.at[6])
    out_copy.start()
    parts = end_of(steps)
    for a in range(2):
        sg_out[:, a * HALF : (a + 1) * HALF] = parts[a]
    for copy in begun:
        copy.wait_send()
    out_copy.wait()


def copies_of(sizes):
    Y, XL, Z, XH, C = sizes
    N, NQ = XL * XH, Y * XL
    plain = (Z - 1) + 4 * (N - 1) + 1
    beside = (Z - 1) + 2 * (N - 1) + 1
    return 4 * plain + 2 * beside + 2 * (NQ - 1)


def shards(sizes, tokens, slot_embed, expert_in, expert_out, out_grad):
    Y, XL, Z, XH, C = sizes
    N, NQ = XL * XH, Y * XL
    T, D = tokens.shape
    S = slot_embed.shape[1] * Z * XH * C
    W = D // NQ
    H = W // 2
    vm = pltpu.VMEM

    def reduce_buffers(w):
        return [
            vm((2, C, N * N, Z, 8, w), BF16),
            vm((2, N * N, Z, 8, w), BF16),
            vm((2, N, Z, 8, w), BF16),
            vm((2, Z, 8, w), BF16),
            vm((2, N * N, Z, 8, w), BF16),
            vm((2, N - 1, N, Z, 8, w), BF16),
            vm((2, N - 1, Z, 8, w), BF16),
            vm((Z - 1, 2, 8, w), BF16),
        ]

    n = copies_of(sizes)
    scratch = [
        vm((T, D), BF16), vm((T, D), BF16), vm(expert_in.shape, BF16), vm(expert_out.shape, BF16),
        vm((D, T), BF16), vm((D, T), BF16), vm((S, D), BF16), vm((S, D), BF16),
        vm((S, T), F32), vm((S, T), F32), vm((8, 128), F32), vm((S, T), F32), vm((S, T), F32),
        vm((T, 2 * S), BF16), vm((T, D), BF16), vm((S, 128), F32),
        vm((2, Y, XL, C, XH, Z, 8, H), BF16), vm((2, Y, XL, C, XH, Z, 8, W), BF16),
        *reduce_buffers(W), *reduce_buffers(H),
        vm((5, 8, S), F32), vm((1, 8, S), F32), vm((N - 1, 8, S), F32), vm((N - 1, 8, S), F32), vm((Z - 1, 8, S), F32),
        vm((4, 8, S), F32), vm((Z - 1, 8, S), F32), vm((N - 1, 8, S), F32), vm((N - 1, 8, S), F32), vm((1, 8, S), F32),
        vm((NQ, 2, 8, W), BF16), vm((NQ, 2, 8, W), BF16), vm((NQ - 1, 2, 8, W), BF16),
        pltpu.SemaphoreType.DMA((7,)), pltpu.SemaphoreType.DMA((n,)), pltpu.SemaphoreType.DMA((n,)),
    ]
    hbm = pl.BlockSpec(memory_space=pl.ANY)
    tok_grad, slot_grad = pl.pallas_call(
        functools.partial(kernel, sizes),
        out_shape=(jax.ShapeDtypeStruct((T, D), BF16), jax.ShapeDtypeStruct((8, W), F32)),
        in_specs=[hbm] * 5,
        out_specs=(hbm, pl.BlockSpec(memory_space=pltpu.VMEM)),
        scratch_shapes=scratch,
        compiler_params=pltpu.CompilerParams(collective_id=0, has_side_effects=True),
        name="soft_moe",
    )(tokens, slot_embed.T, expert_in, expert_out, out_grad)
    return tok_grad, slot_grad.T


SIZES = (4, 2, 8, 2, 2)


def solution(mesh, sizes=SIZES):
    torus = Mesh(mesh.devices.reshape(sizes), AXES)
    placed = (
        P(SEQ_EXP, None),
        P(None, EXP),
        P(EXP, None, SEQ),
        P(EXP, SEQ, None),
        P(SEQ_EXP, None),
    )
    return jax.shard_map(
        functools.partial(shards, sizes),
        mesh=torus,
        in_specs=placed,
        out_specs=(P(SEQ_EXP, None), P(SEQ, EXP)),
        check_vma=False,
    )
```

time: 534 us -> 106 us (0.20)
  waiting for transfers between devices: 343 us -> 0 us
  blocking collectives: 106 us -> 0 us
  Pallas kernels: 0 us -> 99.8 us
  matrix products: 30.2 us -> 0 us
  starting transfers between devices: 28.9 us -> 0 us
  between operations: 13.9 us -> 0.64 us
    all_gather x3 -> x0, waiting for transfers between devices: 182 us -> none  [the longest x1 84.8 us: shards(): slot_table = lax.all_gather(slot_embed, EXP, axis=1, tiled=True)]
    all_to_all x6 -> x0, waiting for transfers between devices: 161 us -> none  [the longest x4 144 us: sum_at_owner(): blocks = lax.all_to_all(split_up(x, dim, size), axis, 0, 0, tiled=True)]
    pallas_call x0 -> x1, Pallas kernels: none -> 99.8 us  [shards(): pl.pallas_call(functools.partial(kernel, sizes), out_shape=(jax.ShapeDtyp...]
    all_gather x5 -> x0, blocking collectives: 44.8 us -> none  [collected_together(): both, at, found = (lax.all_gather(jnp.concatenate(lines), axis), 0, {})]
    psum x5 -> x0, blocking collectives: 40.3 us -> none  [one_axis_at_a_time(): return functools.reduce(lax.psum, axes, x)]
    dot_general x11 -> x0, matrix products: 30.2 us -> none  [the longest x3 7.07 us: contract_cols(): lax.dot_general(left, right, (((1,), (1,)), ((), ())), preferred_element_...]
    all_to_all x6 -> x0, starting transfers between devices: 28.8 us -> none  [the longest x4 21.1 us: sum_at_owner(): blocks = lax.all_to_all(split_up(x, dim, size), axis, 0, 0, tiled=True)]
    all_to_all x2 -> x0, blocking collectives: 21.1 us -> none  [from_everyone(): return lax.all_to_all(copies, axis, split_axis=0, concat_axis=0, tiled=True)]
  transfers between devices with their start and end apart: 9 -> 0, of which waited for: 9 -> 0; matrix products, arithmetic and copies ran while one was open for 3% -> 0% of each run, Pallas kernels for 0% -> 0%
where the time goes in v1:
time: 106 us; the launch traced here: 104 us
  Pallas kernels  99.8 us (94%)
  local copies, waits for them, and re-layouts  3.6 us (3%)
    pallas_call x1, Pallas kernels, shards(): pl.pallas_call(functools.partial(kernel, sizes), out_shape=(jax.ShapeDtyp...  99.8 us
    unnamed x2, local copies, waits for them, and re-layouts  3.6 us

profile of v1, /device:TPU:1, one launch (start us, length us, event | category | flops | bytes accessed | tf_op | source)
XLA Modules:
  0.0 104.0 jit_solution(11694163462501585895)
XLA Ops:
  0.6 99.8 %soft_moe.1 = (bf16[256,2048]{1,0:T(8,128)(2,1)}, f32[8,256]{1,0:T(8,128)}) custom-call(bf16[256,2048]{1,0:T(8,128)(2,1)} %tok_hbm.1, bf16[8,2048]{1,0:T(8,128)(2,1)} %bitcast.2, bf16[2,2048,512]{2,1,0:T(8,128)(2,1)} %win_hbm.1, bf16[2,512,2048]{2,1,0:T(8,128)(2,1)} %wout_hbm.1, bf16[256,2048]{1,0:T(8,128)(2,1)} %og_hbm.1), custom_call_target="tpu_custom_call" | custom-call | tf_op jit(solution)/shard_map/soft_moe/pallas_call | solution.py:453
  100.4 2.3 %copy.9 = bf16[256,2048]{1,0:T(8,128)(2,1)} copy(bf16[256,2048]{1,0:T(8,128)(2,1)} %get-tuple-element.8) | data formatting | bytes 2097152
  102.7 1.3 %copy.10 = f32[256,8]{0,1:T(8,128)} copy(f32[256,8]{0,1:T(8,128)} %bitcast.3) | data formatting | bytes 16384

commit v2 on v1

v2 whole, which is shorter than its diff:
```python
import functools

import jax
import jax.numpy as jnp
from jax import lax
from jax.experimental import pallas as pl
from jax.experimental.pallas import tpu as pltpu
from jax.sharding import Mesh
from jax.sharding import PartitionSpec as P

EXP = ("exp_0", "exp_1", "exp_2")
SEQ = ("seq_0", "seq_1")
SEQ_EXP = ("seq_0", "seq_1", "exp_0", "exp_1", "exp_2")
AXES = SEQ_EXP
F32, BF16 = jnp.float32, jnp.bfloat16
ROOT = 0.7978845608028654


def rows_dot(left, right):
    return lax.dot_general(left, right, (((1,), (0,)), ((), ())), preferred_element_type=F32)


def cols_dot(left, right):
    return lax.dot_general(left, right, (((1,), (1,)), ((), ())), preferred_element_type=F32)


def gelu_and_slope(v):
    t = jnp.tanh(ROOT * (v + 0.044715 * (v * v * v)))
    value = 0.5 * v * (1.0 + t)
    slope = 0.5 * (1.0 + t) + 0.5 * v * (1.0 - t * t) * (ROOT * (1.0 + 3.0 * 0.044715 * (v * v)))
    return value, slope


def flat(block):
    block = block.astype(F32)
    return block.reshape(-1, block.shape[-1])


def kernel(
    sizes,
    tok_hbm, slot_hbm, win_hbm, wout_hbm, og_hbm,
    tg, sg_out,
    tok, og, win, wout, tok_t, og_t, pair, logits, weight, comb_g, disp_g, both, tg_send, tg_rec,
    gath_a, gath_d,
    pb, pb2, pb3, rb1, rb2, rbz,
    pg, pg2, pg3, rg1, rg2, rgz,
    stat, stat_1, stat_2, stat_z, factor,
    cen, cen_z, cen_1, cen_2,
    seq_in, seq_out, seq_rec, line, line_rec,
    local_sem, send_sem, recv_sem,
):
    Y, XL, Z, XH, C = sizes
    N, NQ = XL * XH, Y * XL
    assert Y == N and C == 2 and XL == 2 and XH == 2
    S = XH * Z * 8
    T = tok.shape[0] // 2
    W = tok.shape[1] // NQ
    HALF = W // 2
    ZR = Z * 8
    y, xl, z, xh, c = (lax.axis_index(name) for name in AXES)
    x, q = xh * XL + xl, y * XL + xl
    rem, div = lax.rem, lax.div

    def z_to(i):
        k = rem(z + i, Z)
        return k, {"exp_0": k}

    def y_to(i):
        k = rem(y + i, N)
        return k, {"seq_0": k}

    def x_to(i):
        k = rem(x + i, N)
        return k, {"exp_1": div(k, XL), "seq_1": rem(k, XL)}

    def seq_to(dy, dl):
        ky, kl = rem(y + dy, N), rem(xl + dl, XL)
        return ky * XL + kl, {"seq_0": ky, "seq_1": kl}

    def seq_from(dy, dl):
        return rem(y + N - dy, N) * XL + rem(xl + dl, XL)

    def by_x(k):
        return rem(k, XL) * Y + div(k, XL)

    other = {"exp_2": 1 - c}
    far_first = (2, 1, 3)
    seq_far_first = ((2, 1), (2, 0), (1, 1), (3, 1), (1, 0), (3, 0), (0, 1))
    MESH = pl.DeviceIdType.MESH
    count = [0]
    begun = []

    def send(src, dst, device):
        k = count[0]
        count[0] += 1
        copy = pltpu.make_async_remote_copy(
            src_ref=src, dst_ref=dst, send_sem=send_sem.at[k], recv_sem=recv_sem.at[k],
            device_id=device, device_id_type=MESH,
        )
        copy.start()
        begun.append(copy)
        return copy

    def arrive(copies):
        for copy in copies:
            copy.wait_recv()

    def columns(k, width):
        return pl.ds(pl.multiple_of(k * width, width), width)

    mine, theirs = pl.ds(0, T), pl.ds(T, T)
    first = [
        pltpu.make_async_copy(
            slot_hbm.at[:, columns(start, HALF)],
            gath_a.at[a, y, xl, xh, z],
            local_sem.at[a],
        )
        for a, start in ((0, y * XL + xl), (1, NQ + xl * Y + y))
    ]
    big = [
        pltpu.make_async_copy(src, dst, local_sem.at[2 + k])
        for k, (src, dst) in enumerate(
            ((tok_hbm, tok.at[mine]), (og_hbm, og.at[mine]), (win_hbm, win), (wout_hbm, wout))
        )
    ]
    for copy in first + big:
        copy.start()

    barrier = pltpu.get_barrier_semaphore()
    partners = [z_to(i)[1] for i in range(1, Z)]
    partners += [y_to(i)[1] for i in range(1, N)]
    partners += [x_to(i)[1] for i in range(1, N)]
    partners += [seq_to(*step)[1] for step in seq_far_first]
    partners += [other]
    for device in partners:
        pl.semaphore_signal(barrier, inc=1, device_id=device, device_id_type=MESH)
    for copy in first:
        copy.wait()
    pl.semaphore_wait(barrier, len(partners))

    def gather(buf, beside=None):
        moves = [send(buf.at[:, y, xl, xh, z], buf.at[:, y, xl, xh, z], z_to(i)[1]) for i in (4, 3, 5, 2, 6, 1, 7) if i < Z]
        if beside:
            own, over_z, over_1, over_2 = beside
            moves += [send(own.at[0], over_z.at[i - 1], z_to(i)[1]) for i in range(1, Z)]
        yield
        arrive(moves)
        moves = []
        for i in far_first:
            moves.append(send(buf.at[0, y, xl, xh], buf.at[0, y, xl, xh], x_to(i)[1]))
            moves.append(send(buf.at[1, y, xl, xh], buf.at[1, y, xl, xh], y_to(i)[1]))
        if beside:
            total = own[0]
            for i in range(1, Z):
                total += over_z[i - 1]
            own[1] = total
            moves += [send(own.at[1], over_1.at[i - 1], x_to(i)[1]) for i in range(1, N)]
        yield
        arrive(moves)
        moves = {}
        for i in far_first:
            moves[0, i] = [send(buf.at[0, y], buf.at[0, y], y_to(i)[1])]
            moves[1, i] = [send(buf.at[1, :, xl, xh], buf.at[1, :, xl, xh], x_to(i)[1])]
        if beside:
            total = own[1]
            for i in range(1, N):
                total += over_1[i - 1]
            own[2] = total
            moves[2, 0] = [send(own.at[2], over_2.at[i - 1], y_to(i)[1]) for i in range(1, N)]
        yield moves

    lines = lax.broadcasted_iota(jnp.int32, (8, S), 0)

    def merge(entries, k):
        top = entries[0][0:1]
        for entry in entries[1:]:
            top = jnp.maximum(top, entry[0:1])
        scales = [jnp.exp(entry[0:1] - top) for entry in entries]
        total = entries[0][1:2] * scales[0]
        for entry, scale in zip(entries[1:], scales[1:]):
            total += entry[1:2] * scale
        turned = jnp.zeros((8, S), F32)
        for j, scale in enumerate(scales):
            turned = jnp.where(lines == j, scale, turned)
        factor[k] = jnp.concatenate([turned, jnp.zeros((120, S), F32)], axis=0).T
        return jnp.where(lines == 0, top, jnp.where(lines == 1, total, 0.0))

    def joined(parts, scale, row, rows):
        total = None
        for k, part in enumerate(parts):
            part = flat(part)
            if scale is not None:
                part = part * factor[scale, pl.ds(pl.multiple_of(row, 8), rows), k : k + 1]
            total = part if total is None else total + part
        return total

    def reduce(p, s2, s3, r1, r2, rz, moves, stats=None):
        w = p.shape[-1]
        scaled = stats is not None
        if scaled:
            arrive(stats)
            stat[1] = merge([stat[0]] + [stat_1[i] for i in range(N - 1)], 0)
            stats = [send(stat.at[1], stat_2.at[i - 1], x_to(i)[1]) for i in far_first]
        arrive(moves)

        def second_sum(b, _):
            for a, me in ((0, y), (1, x)):
                parts = [p[a, me, b]] + [r1[a, i, b] for i in range(N - 1)]
                total = joined(parts, 0 if scaled and a == 0 else None, div(b, XL) * ZR, ZR)
                s2[a, b] = total.reshape(Z, 8, w).astype(BF16)
            return 0

        lax.fori_loop(0, N, second_sum, 0)
        moves = []
        for i in far_first:
            k, device = x_to(i)
            moves.append(send(s2.at[0, k], r2.at[0, i - 1], device))
            k, device = y_to(i)
            moves.append(send(s2.at[1, k], r2.at[1, i - 1], device))
        yield
        if scaled:
            arrive(stats)
            stat[2] = merge([stat[1]] + [stat_2[i] for i in range(N - 1)], 1)
            stats = [send(stat.at[2], stat_z.at[i - 1], z_to(i)[1]) for i in range(1, Z)]
        arrive(moves)
        for a, me in ((0, x), (1, y)):
            parts = [s2[a, me]] + [r2[a, i] for i in range(N - 1)]
            total = joined(parts, 1 if scaled and a == 0 else None, xh * ZR, ZR)
            s3[a] = total.reshape(Z, 8, w).astype(BF16)
        moves = []
        for i in (4, 3, 5, 2, 6, 1, 7):
            if i < Z:
                k, device = z_to(i)
                moves.append(send(s3.at[:, k], rz.at[i - 1], device))
        if scaled:
            arrive(stats)
            final = merge([stat[2]] + [stat_z[i] for i in range(Z - 1)], 2)
            factor[3] = jnp.concatenate([final, jnp.zeros((120, S), F32)], axis=0).T
        yield
        arrive(moves)
        result = []
        for a in range(2):
            parts = [s3[a, z]] + [rz[i, a] for i in range(Z - 1)]
            result.append(joined(parts, 2 if scaled and a == 0 else None, own_row, 8))
        yield result

    def end_of(steps):
        last = None
        for last in steps:
            pass
        return last

    own_row = pl.multiple_of(xh * ZR + z * 8, 8)

    def turn(source, target, half):
        target[:, half * T : half * T + T] = source[half * T : half * T + T].T

    steps = gather(gath_a)
    next(steps)
    swaps = [send(tok_hbm, tok.at[theirs], other)]
    big[0].wait()
    turn(tok, tok_t, 0)
    next(steps)
    swaps.append(send(og_hbm, og.at[theirs], other))
    arrive(swaps[:1])
    turn(tok, tok_t, 1)
    last = next(steps)
    logits[...] = jnp.zeros_like(logits)

    def table_by_y(ky):
        span = columns(ky, XL * HALF)
        block = jnp.concatenate([flat(gath_a[0, ky, kl]) for kl in range(XL)], axis=1).astype(BF16)
        pair[S : 2 * S, span] = block
        logits[...] += rows_dot(block, tok_t[span, :])

    def table_by_x(kx):
        kh, kl = div(kx, XL), rem(kx, XL)
        span = pl.ds(pl.multiple_of(NQ * HALF + kl * (Y * HALF), HALF), Y * HALF)
        block = jnp.concatenate([flat(gath_a[1, ky, kl, kh]) for ky in range(Y)], axis=1).astype(BF16)
        pair[pl.ds(pl.multiple_of(S + kh * ZR, ZR), ZR), span] = block
        logits[columns(kh, ZR), :] += rows_dot(block, tok_t[span, :])

    big[1].wait()
    turn(og, og_t, 0)
    arrive(swaps[1:])
    turn(og, og_t, 1)
    table_by_y(y)
    table_by_x(x)
    for i in (1, 3, 2):
        arrive(last[0, i])
        table_by_y(rem(y + N - i, N))
        arrive(last[1, i])
        table_by_x(rem(x + N - i, N))
    lg = logits[...]

    slots_b = jnp.max(lg, axis=0, keepdims=True)
    raised = jnp.exp(lg - slots_b)
    sums_b = jnp.sum(raised, axis=0, keepdims=True)
    wide = lax.broadcasted_iota(jnp.int32, (8, 2 * T), 0)
    line[0] = jnp.where(wide == 0, slots_b, sums_b)
    line_move = send(line.at[0], line_rec.at[0], other)
    top = jnp.max(lg, axis=1, keepdims=True)
    local = jnp.exp(lg - top)
    total = jnp.sum(local, axis=1, keepdims=True)
    lanes = lax.broadcasted_iota(jnp.int32, (S, 128), 1)
    stat[0] = jnp.where(lanes == 0, top, jnp.where(lanes == 1, total, 0.0)).T[0:8]
    stats = [send(stat.at[0], stat_1.at[i - 1], y_to(i)[1]) for i in far_first]
    local_b = local.astype(BF16)

    def place(target, a, ky, kl, values):
        for hh in range(XH):
            block = values[hh * ZR : hh * ZR + ZR].reshape(Z, 8, values.shape[1]).astype(BF16)
            if a == 0:
                target[0, ky, hh * XL + kl] = block
            else:
                target[1, hh * XL + kl, ky] = block

    moves = []
    for i in far_first + (0,):
        ky, device = y_to(i)

        values = rows_dot(local_b, tok[:, columns(ky, XL * W)])
        for kl in range(XL):
            place(pb, 0, ky, kl, values[:, kl * W : (kl + 1) * W])
        if i:
            moves.append(send(pb.at[0, ky], rb1.at[0, i - 1], device))
        if i == 1:
            arrive([line_move])
            got = line_rec[0]
            got = jnp.concatenate([got[:, T:], got[:, :T]], axis=1)
            high = jnp.maximum(slots_b, got[0:1])
            low = jnp.exp(slots_b - high)
            share = low / (sums_b * low + got[1:2] * jnp.exp(got[0:1] - high))
            comb = raised * share
            weight[...] = comb
            comb_b = comb.astype(BF16)
    for near in (0, 1):
        kl = rem(xl + near, XL)

        for pick_y in range(Y // 2):
            values = rows_dot(comb_b, og[:, columns(kl * (Y // 2) + pick_y, 2 * W)])
            for k in range(2):
                place(pb, 1, 2 * pick_y + k, kl, values[:, k * W : (k + 1) * W])
        for i in (1, 3) if near else (2,):
            k, device = x_to(i)
            moves.append(send(pb.at[1, k], rb1.at[1, i - 1], device))
    sum_chunk, grad_chunk = end_of(reduce(pb, pb2, pb3, rb1, rb2, rbz, moves, stats))

    sum_chunk = sum_chunk / factor[3, pl.ds(own_row, 8), 1:2]
    seq_in[q, 0] = sum_chunk.astype(BF16)
    seq_in[q, 1] = grad_chunk.astype(BF16)
    moves = {step: send(seq_in.at[q], seq_in.at[q], seq_to(*step)[1]) for step in seq_far_first}
    big[2].wait()
    big[3].wait()
    upper = lax.broadcasted_iota(jnp.int32, (8, 1), 0) < 4

    def pick(f, g):
        return jnp.where(upper, f, g)

    pre = hid_grad = None
    for step in ((0, 0),) + seq_far_first[::-1]:
        if step != (0, 0):
            arrive([moves[step]])
        k = seq_from(*step)
        slot_b, grad_b = (seq_in[k, a].astype(F32).astype(BF16) for a in range(2))
        more = [rows_dot(slot_b, win[e, columns(k, W), :]) for e in range(2)]
        pre = more if pre is None else [f + g for f, g in zip(pre, more)]
        more = [cols_dot(grad_b, wout[e, :, columns(by_x(k), W)]) for e in range(2)]
        hid_grad = more if hid_grad is None else [f + g for f, g in zip(hid_grad, more)]
    hidden, slope = gelu_and_slope(pick(*pre))
    hidden = hidden.astype(BF16)
    act = (pick(*hid_grad) * slope).astype(BF16)
    moves = []
    for step in seq_far_first + ((0, 0),):
        k, device = seq_to(*step)
        in_part = pick(*(cols_dot(act, win[e, columns(k, W), :]) for e in range(2)))
        out_part = pick(*(rows_dot(hidden, wout[e, :, columns(by_x(k), W)]) for e in range(2)))
        seq_out[k, 0] = in_part.astype(BF16)
        seq_out[k, 1] = out_part.astype(BF16)
        if step != (0, 0):
            moves.append(send(seq_out.at[k], seq_rec.at[step[0] * XL + step[1] - 1], device))
    arrive(moves)
    for a in (1, 0):
        total = seq_out[q, a].astype(F32)
        for i in range(NQ - 1):
            total += seq_rec[i, a].astype(F32)
        gath_d[a, y, xl, xh, z] = total.astype(BF16)
    part = jnp.sum(sum_chunk * total.astype(BF16).astype(F32), axis=1, keepdims=True)
    spots = lax.broadcasted_iota(jnp.int32, (8, S), 1)
    cen[0] = jnp.where(spots == own_row + lines, part, 0.0)
    *_, last = gather(gath_d, (cen, cen_z, cen_1, cen_2))

    comb_g[...] = jnp.zeros_like(comb_g)
    disp_g[...] = jnp.zeros_like(disp_g)

    def back_disp(ky):
        span = columns(ky, XL * W)
        block = jnp.concatenate([flat(gath_d[0, ky, kl]) for kl in range(XL)], axis=1).astype(BF16)
        pair[0:S, span] = block
        disp_g[...] += rows_dot(block, tok_t[span, :])

    def back_comb(kx):
        kh, kl = div(kx, XL), rem(kx, XL)
        block = jnp.concatenate([flat(gath_d[1, ky, kl, kh]) for ky in range(Y)], axis=1).astype(BF16)
        comb_g[columns(kh, ZR), :] += rows_dot(block, og_t[columns(kl, Y * W), :])

    back_comb(x)
    back_disp(y)
    for i in (1, 3, 2):
        arrive(last[1, i])
        back_comb(rem(x + N - i, N))
        if i == 2:
            comb = weight[...]
            comb_grad = comb_g[...]
            mean = jnp.sum(comb * comb_grad, axis=0, keepdims=True)
            line[1] = jnp.broadcast_to(mean, (8, 2 * T))
            line_move = send(line.at[1], line_rec.at[1], other)
        arrive(last[0, i])
        back_disp(rem(y + N - i, N))
    arrive(last[2, 0])
    centre_row = cen[2]
    for i in range(N - 1):
        centre_row += cen_2[i]
    centre = jnp.broadcast_to(jnp.sum(centre_row, axis=0, keepdims=True), (128, S)).T[:, 0:1]
    disp = jnp.exp(logits[...] - factor[3, :, 0:1]) / factor[3, :, 1:2]
    disp_part = disp * (disp_g[...] - centre)
    arrive([line_move])
    got = line_rec[1]
    mean = mean + jnp.concatenate([got[:, T:], got[:, :T]], axis=1)[0:1]
    logit_grad = disp_part + comb * (comb_grad - mean)
    logit_b = logit_grad.astype(BF16)

    moves = []
    for i in far_first + (0,):
        ky, device = y_to(i)

        values = rows_dot(logit_b, tok[:, columns(ky, XL * W)])
        for kl in range(XL):
            for a in range(2):
                place(pg, a, ky, kl, values[:, (2 * kl + a) * HALF : (2 * kl + a + 1) * HALF])
        if i:
            moves.append(send(pg.at[0, ky], rg1.at[0, i - 1], device))
    for i in far_first:
        k, device = x_to(i)
        moves.append(send(pg.at[1, k], rg1.at[1, i - 1], device))
    both[:, 0:S] = disp.T.astype(BF16)
    both[:, S : 2 * S] = logit_grad.T.astype(BF16)

    def their_grads(k, _):
        tg_send[:, columns(k, W)] = rows_dot(both[T : 2 * T], pair[:, columns(k, W)]).astype(BF16)
        return 0

    lax.fori_loop(0, NQ, their_grads, 0)
    tg_move = send(tg_send, tg_rec, other)
    steps = reduce(pg, pg2, pg3, rg1, rg2, rgz, moves)
    next(steps)
    arrive([tg_move])

    def own_grads(k, _):
        span = columns(k, W)
        tg[:, span] = (rows_dot(both[0:T], pair[:, span]) + tg_rec[:, span].astype(F32)).astype(BF16)
        return 0

    lax.fori_loop(0, NQ, own_grads, 0)
    parts = end_of(steps)
    for a in range(2):
        sg_out[:, a * HALF : (a + 1) * HALF] = parts[a]
    for copy in begun:
        copy.wait_send()


def copies_of(sizes):
    Y, XL, Z, XH, C = sizes
    N, NQ = XL * XH, Y * XL
    return 4 * (Z - 1 + 4 * (N - 1)) + 2 * (Z - 1 + 2 * (N - 1)) + 2 * (NQ - 1) + 5


def shards(sizes, tokens, slot_embed, expert_in, expert_out, out_grad):
    Y, XL, Z, XH, C = sizes
    N, NQ = XL * XH, Y * XL
    T, D = tokens.shape
    S = slot_embed.shape[1] * Z * XH
    W = D // NQ
    H = W // 2
    vm = pltpu.VMEM

    def reduce_buffers(w):
        return [
            vm((2, N, N, Z, 8, w), BF16),
            vm((2, N, Z, 8, w), BF16),
            vm((2, Z, 8, w), BF16),
            vm((2, N - 1, N, Z, 8, w), BF16),
            vm((2, N - 1, Z, 8, w), BF16),
            vm((Z - 1, 2, 8, w), BF16),
        ]

    n = copies_of(sizes)
    scratch = [
        vm((2 * T, D), BF16), vm((2 * T, D), BF16), vm(expert_in.shape, BF16), vm(expert_out.shape, BF16),
        vm((D, 2 * T), BF16), vm((D, 2 * T), BF16), vm((2 * S, D), BF16),
        vm((S, 2 * T), F32), vm((S, 2 * T), F32), vm((S, 2 * T), F32), vm((S, 2 * T), F32),
        vm((2 * T, 2 * S), BF16), vm((T, D), BF16), vm((T, D), BF16),
        vm((2, Y, XL, XH, Z, 8, H), BF16), vm((2, Y, XL, XH, Z, 8, W), BF16),
        *reduce_buffers(W), *reduce_buffers(H),
        vm((3, 8, S), F32), vm((N - 1, 8, S), F32), vm((N - 1, 8, S), F32), vm((Z - 1, 8, S), F32), vm((4, S, 128), F32),
        vm((3, 8, S), F32), vm((Z - 1, 8, S), F32), vm((N - 1, 8, S), F32), vm((N - 1, 8, S), F32),
        vm((NQ, 2, 8, W), BF16), vm((NQ, 2, 8, W), BF16), vm((NQ - 1, 2, 8, W), BF16),
        vm((2, 8, 2 * T), F32), vm((2, 8, 2 * T), F32),
        pltpu.SemaphoreType.DMA((6,)), pltpu.SemaphoreType.DMA((n,)), pltpu.SemaphoreType.DMA((n,)),
    ]
    hbm = pl.BlockSpec(memory_space=pl.ANY)
    tok_grad, slot_grad = pl.pallas_call(
        functools.partial(kernel, sizes),
        out_shape=(pltpu.VMEM((T, D), BF16), pltpu.VMEM((8, W), F32)),
        in_specs=[hbm] * 5,
        out_specs=(pl.BlockSpec(memory_space=pltpu.VMEM), pl.BlockSpec(memory_space=pltpu.VMEM)),
        scratch_shapes=scratch,
        compiler_params=pltpu.CompilerParams(collective_id=0, has_side_effects=True),
        name="soft_moe",
    )(tokens, slot_embed.T, expert_in, expert_out, out_grad)
    return tok_grad, slot_grad.T


SIZES = (4, 2, 8, 2, 2)


def solution(mesh, sizes=SIZES):
    torus = Mesh(mesh.devices.reshape(sizes), AXES)
    placed = (
        P(SEQ_EXP, None),
        P(None, EXP),
        P(EXP, None, SEQ),
        P(EXP, SEQ, None),
        P(SEQ_EXP, None),
    )
    return jax.shard_map(
        functools.partial(shards, sizes),
        mesh=torus,
        in_specs=placed,
        out_specs=(P(SEQ_EXP, None), P(SEQ, EXP)),
        check_vma=False,
    )
```

time: 106 us -> 90.1 us (0.85); the launches traced: 104 us -> 90 us
  Pallas kernels: 99.8 us -> 87.8 us
  local copies, waits for them, and re-layouts: 3.6 us -> 1.57 us
    pallas_call x1, Pallas kernels: 99.8 us -> 87.8 us  [shards(): pl.pallas_call(functools.partial(kernel, sizes), out_shape=(pltpu.VMEM((T...]
    unnamed x2, local copies, waits for them, and re-layouts: 3.6 us -> 1.57 us
where the time goes in v2:
time: 90.1 us; the launch traced here: 90 us
  Pallas kernels  87.8 us (97%)
  local copies, waits for them, and re-layouts  1.57 us (2%)
    pallas_call x1, Pallas kernels, shards(): pl.pallas_call(functools.partial(kernel, sizes), out_shape=(pltpu.VMEM((T...  87.8 us

profile of v2, /device:TPU:1, one launch (start us, length us, event | category | flops | bytes accessed | tf_op | source)
XLA Modules:
  0.0 90.0 jit_solution(6529030609231636805)
XLA Ops:
  0.6 87.8 %soft_moe.1 = (bf16[256,2048]{1,0:T(8,128)(2,1)S(1)}, f32[8,256]{1,0:T(8,128)S(1)}) custom-call(bf16[256,2048]{1,0:T(8,128)(2,1)} %tok_hbm.1, bf16[8,2048]{1,0:T(8,128)(2,1)} %bitcast.3, bf16[2,2048,512]{2,1,0:T(8,128)(2,1)} %win_hbm.1, bf16[2,512,2048]{2,1,0:T(8,128)(2,1)} %wout_hbm.1, bf16[256,2048]{1,0:T(8,128)(2,1)} %og_hbm.1), custom_call_target="tpu_custom_call" | custom-call | tf_op jit(solution)/shard_map/soft_moe/pallas_call | solution.py:512
  88.4 1.0 %copy.9 = bf16[256,2048]{1,0:T(8,128)(2,1)} copy(bf16[256,2048]{1,0:T(8,128)(2,1)S(1)} %get-tuple-element.6) | data formatting | bytes 2097152
  89.4 0.6 copy.10

commit v3 on v2

v3 whole, which is shorter than its diff:
```python
import functools

import jax
import jax.numpy as jnp
from jax import lax
from jax.experimental import pallas as pl
from jax.experimental.pallas import tpu as pltpu
from jax.sharding import Mesh
from jax.sharding import PartitionSpec as P

EXP = ("exp_0", "exp_1", "exp_2")
SEQ = ("seq_0", "seq_1")
SEQ_EXP = ("seq_0", "seq_1", "exp_0", "exp_1", "exp_2")
AXES = SEQ_EXP
F32, BF16 = jnp.float32, jnp.bfloat16
ROOT = 0.7978845608028654


def rows_dot(left, right):
    return lax.dot_general(left, right, (((1,), (0,)), ((), ())), preferred_element_type=F32)


def cols_dot(left, right):
    return lax.dot_general(left, right, (((1,), (1,)), ((), ())), preferred_element_type=F32)


def gelu_and_slope(v):
    t = jnp.tanh(ROOT * (v + 0.044715 * (v * v * v)))
    value = 0.5 * v * (1.0 + t)
    slope = 0.5 * (1.0 + t) + 0.5 * v * (1.0 - t * t) * (ROOT * (1.0 + 3.0 * 0.044715 * (v * v)))
    return value, slope


def flat(block):
    block = block.astype(F32)
    return block.reshape(-1, block.shape[-1])


def kernel(
    sizes,
    tok_hbm, slot_hbm, win_hbm, wout_hbm, og_hbm,
    tg, sg_out,
    tok, og, win, wout, tok_t, og_t, pair, logits, weight, comb_g, disp_g, both, tg_send, tg_rec,
    own_a, own_d, gath_a, gath_d,
    pb, pb2, pb3, rb1, rb2, rbz,
    pg, pg2, pg3, rg1, rg2, rgz,
    stat, stat_p, stat_z, factor, scale_out, scale_in,
    cen, cen_z, cen_p,
    seq_in, seq_out, seq_rec, line, line_rec,
    local_sem, send_sem, recv_sem,
):
    Y, XL, Z, XH, C = sizes
    N, NQ = XL * XH, Y * XL
    assert Y == N and C == 2 and XL == 2 and XH == 2
    S = XH * Z * 8
    T = tok.shape[0] // 2
    W = tok.shape[1] // NQ
    HALF = W // 2
    ZR = Z * 8
    y, xl, z, xh, c = (lax.axis_index(name) for name in AXES)
    x, q = xh * XL + xl, y * XL + xl
    rem, div = lax.rem, lax.div

    def z_to(i):
        k = rem(z + i, Z)
        return k, {"exp_0": k}

    def owner_to(i):
        k = rem(z + i, Z)
        return k, {"exp_0": k, "exp_2": 1 - c}

    def y_to(i):
        k = rem(y + i, N)
        return k, {"seq_0": k}

    def x_to(i):
        k = rem(x + i, N)
        return k, {"exp_1": div(k, XL), "seq_1": rem(k, XL)}

    def plane_to(dy, dx):
        kx = rem(x + dx, N)
        return {"seq_0": rem(y + dy, N), "exp_1": div(kx, XL), "seq_1": rem(kx, XL)}

    def seq_to(dy, dl):
        ky, kl = rem(y + dy, N), rem(xl + dl, XL)
        return ky * XL + kl, {"seq_0": ky, "seq_1": kl}

    def seq_from(dy, dl):
        return rem(y + N - dy, N) * XL + rem(xl + dl, XL)

    def by_x(k):
        return rem(k, XL) * Y + div(k, XL)

    other = {"exp_2": 1 - c}
    far_first = (2, 1, 3)
    z_far_first = sorted(range(Z), key=lambda i: -min(i, Z - i))
    plane = [(dy, dx) for dy in (2, 1, 3, 0) for dx in (2, 1, 3, 0) if dy or dx]
    seq_far_first = ((2, 1), (2, 0), (1, 1), (3, 1), (1, 0), (3, 0), (0, 1))
    MESH = pl.DeviceIdType.MESH
    groups, over = [], [0]

    def group(whole):
        groups.append(whole)
        return len(groups) - 1

    def send(k, src, dst, device):
        pltpu.make_async_remote_copy(
            src_ref=src, dst_ref=dst, send_sem=send_sem.at[k], recv_sem=recv_sem.at[k],
            device_id=device, device_id_type=MESH,
        ).start()

    def arrive(*which):
        for k in which:
            pltpu.make_async_copy(groups[k], groups[k], recv_sem.at[k]).wait()

    def sent(n):
        for k in range(over[0], n):
            pltpu.make_async_copy(groups[k], groups[k], send_sem.at[k]).wait()
        over[0] = max(n, over[0])

    def columns(k, width):
        return pl.ds(pl.multiple_of(k * width, width), width)

    mine, theirs = pl.ds(0, T), pl.ds(T, T)
    first = [
        pltpu.make_async_copy(
            slot_hbm.at[:, columns(start, HALF)],
            own_a.at[a],
            local_sem.at[a],
        )
        for a, start in ((0, y * XL + xl), (1, NQ + xl * Y + y))
    ]
    big = [
        pltpu.make_async_copy(src, dst, local_sem.at[2 + k])
        for k, (src, dst) in enumerate(
            ((tok_hbm, tok.at[mine]), (og_hbm, og.at[mine]), (win_hbm, win), (wout_hbm, wout))
        )
    ]
    for copy in first + big:
        copy.start()

    barrier = pltpu.get_barrier_semaphore()
    partners = [z_to(i)[1] for i in range(1, Z)] + [owner_to(i)[1] for i in range(1, Z)]
    partners += [plane_to(*step) for step in plane]
    partners += [other]
    for device in partners:
        pl.semaphore_signal(barrier, inc=1, device_id=device, device_id_type=MESH)
    for copy in first:
        copy.wait()
    pl.semaphore_wait(barrier, len(partners))

    def gather(block, buf, beside=None):
        along = [group(buf.at[:, y, xl, xh])]
        for i in z_far_first:
            send(along[0], block, buf.at[:, y, xl, xh, z], owner_to(i)[1])
        if beside:
            own, over_z, over_plane = beside
            along.append(group(over_z))
            for i in z_far_first:
                send(along[1], own.at[0], over_z.at[i], owner_to(i)[1])
        yield
        arrive(*along)
        hops = {}
        for i in far_first:
            hops[i] = group(buf.at[:, y, xl, xh])
            send(hops[i], buf.at[0, y, xl, xh], buf.at[0, y, xl, xh], x_to(i)[1])
            send(hops[i], buf.at[1, y, xl, xh], buf.at[1, y, xl, xh], y_to(i)[1])
        last = [group(buf.at[:, 0 : N - 1])]

        def pass_on(j):
            kx = rem(x + N - j, N)
            part = buf.at[0, y, rem(kx, XL), div(kx, XL)]
            for i in far_first:
                send(last[0], part, part, y_to(i)[1])
            part = buf.at[1, rem(y + N - j, N), xl, xh]
            for i in far_first:
                send(last[0], part, part, x_to(i)[1])

        pass_on(0)
        if beside:
            total = over_z[0]
            for i in range(1, Z):
                total += over_z[i]
            own[1] = total
            last.append(group(over_plane))
            for n, step in enumerate(plane):
                send(last[1], own.at[1], over_plane.at[n], plane_to(*step))
        yield
        for j in (1, 3, 2):
            arrive(hops[j])
            pass_on(j)
        yield last

    lines = lax.broadcasted_iota(jnp.int32, (8, S), 0)

    def merge(entries):
        top = entries[0][0]
        for entry in entries[1:]:
            top = jnp.maximum(top, entry[0])
        scales = [jnp.exp(entry[0] - top) for entry in entries]
        total = entries[0][1] * scales[0]
        for entry, scale in zip(entries[1:], scales[1:]):
            total += entry[1] * scale
        return (top, total), scales

    def upright(rows):
        turned = jnp.zeros((16, S), F32)
        tall = lax.broadcasted_iota(jnp.int32, (16, S), 0)
        for k, row in enumerate(rows):
            turned = jnp.where(tall == k, row, turned)
        return jnp.concatenate([turned, jnp.zeros((112, S), F32)], axis=0).T

    def joined(parts, scale, row, rows):
        total = None
        for k, part in enumerate(parts):
            part = flat(part)
            if scale is not None:
                part = part * scale[pl.ds(pl.multiple_of(row, 8), rows), k : k + 1]
            total = part if total is None else total + part
        return total

    def reduce(p, s2, s3, r1, r2, rz, moves, stats=None):
        w = p.shape[-1]
        scaled = stats is not None
        if scaled:
            arrive(*stats)
            stat_of = {(0, 0): stat[0]}
            for n, step in enumerate(plane):
                stat_of[step] = stat_p[n]
            by_y = [merge([(e[0:1], e[1:2]) for e in (stat_of[i, j] for i in range(N))]) for j in range(N)]
            merged, across = merge([joint for joint, _ in by_y])
            stat[1] = jnp.where(lines == 0, merged[0], merged[1])
            stats = [group(stat_z)]
            for i in z_far_first:
                if i:
                    send(stats[0], stat.at[1], stat_z.at[i - 1], z_to(i)[1])
            factor[0] = upright(by_y[0][1])
            factor[1] = upright(across)
        later = [group(r2)]
        for j in far_first + (0,):
            for a, me, (b, device) in ((0, y, x_to(j)), (1, x, y_to(j))):
                arrive(moves[a, j])
                parts = [p[a, me, b]] + [r1[a, i, b] for i in range(N - 1)]
                total = joined(parts, factor.at[0] if scaled and a == 0 else None, div(b, XL) * ZR, ZR)
                s2[a, b] = total.reshape(Z, 8, w).astype(BF16)
                if j:
                    send(later[0], s2.at[a, b], r2.at[a, j - 1], device)
        moves = later
        yield
        if scaled:
            arrive(*stats)
            entries = [stat[1]] + [stat_z[i] for i in range(Z - 1)]
            merged, across = merge([(e[0:1], e[1:2]) for e in entries])
            scale_out[...] = upright(across + list(merged))
            scale_move = group(scale_in)
            send(scale_move, scale_out, scale_in, other)
        arrive(*moves)
        for a, me in ((0, x), (1, y)):
            parts = [s2[a, me]] + [r2[a, i] for i in range(N - 1)]
            total = joined(parts, factor.at[1] if scaled and a == 0 else None, xh * ZR, ZR)
            s3[a] = total.reshape(Z, 8, w).astype(BF16)
        moves = [group(rz)]
        for i in z_far_first:
            k, device = owner_to(i)
            send(moves[0], s3.at[:, k], rz.at[i], device)
        if scaled:
            moves.append(scale_move)
        yield
        arrive(*moves)
        result = []
        for a in range(2):
            parts = [rz[i, a] for i in range(Z)]
            result.append(joined(parts, scale_in if scaled and a == 0 else None, own_row, 8))
        yield result

    def spread(p, r1, a):
        first_to, then_to = (y_to, x_to) if a == 0 else (x_to, y_to)
        moves = {}
        for j in far_first + (0,):
            b = then_to(j)[0]
            moves[a, j] = group(r1.at[a, :, b])
            for i in far_first:
                k, device = first_to(i)
                send(moves[a, j], p.at[a, k, b], r1.at[a, i - 1, b], device)
        return moves

    def end_of(steps):
        last = None
        for last in steps:
            pass
        return last

    own_row = pl.multiple_of(xh * ZR + z * 8, 8)

    def turn(source, target, half):
        target[:, half * T : half * T + T] = source[half * T : half * T + T].T

    steps = gather(own_a, gath_a)
    next(steps)
    swaps = [group(tok.at[theirs]), group(og.at[theirs])]
    send(swaps[0], tok_hbm, tok.at[theirs], other)
    big[0].wait()
    turn(tok, tok_t, 0)
    next(steps)
    send(swaps[1], og_hbm, og.at[theirs], other)
    arrive(swaps[0])
    turn(tok, tok_t, 1)
    last = next(steps)
    logits[...] = jnp.zeros_like(logits)

    def table_by_y(ky):
        span = columns(ky, XL * HALF)
        block = jnp.concatenate([flat(gath_a[0, ky, kl]) for kl in range(XL)], axis=1).astype(BF16)
        pair[S : 2 * S, span] = block
        logits[...] += rows_dot(block, tok_t[span, :])

    def table_by_x(kx):
        kh, kl = div(kx, XL), rem(kx, XL)
        span = pl.ds(pl.multiple_of(NQ * HALF + kl * (Y * HALF), HALF), Y * HALF)
        block = jnp.concatenate([flat(gath_a[1, ky, kl, kh]) for ky in range(Y)], axis=1).astype(BF16)
        pair[pl.ds(pl.multiple_of(S + kh * ZR, ZR), ZR), span] = block
        logits[columns(kh, ZR), :] += rows_dot(block, tok_t[span, :])

    big[1].wait()
    turn(og, og_t, 0)
    arrive(swaps[1])
    turn(og, og_t, 1)
    table_by_y(y)
    table_by_x(x)
    arrive(*last)
    for i in far_first:
        table_by_y(rem(y + N - i, N))
        table_by_x(rem(x + N - i, N))
    lg = logits[...]

    slots_b = jnp.max(lg, axis=0, keepdims=True)
    raised = jnp.exp(lg - slots_b)
    sums_b = jnp.sum(raised, axis=0, keepdims=True)
    wide = lax.broadcasted_iota(jnp.int32, (8, 2 * T), 0)
    line[0] = jnp.where(wide == 0, slots_b, sums_b)
    line_move = group(line_rec.at[0])
    send(line_move, line.at[0], line_rec.at[0], other)
    top = jnp.max(lg, axis=1, keepdims=True)
    local = jnp.exp(lg - top)
    total = jnp.sum(local, axis=1, keepdims=True)
    lanes = lax.broadcasted_iota(jnp.int32, (S, 128), 1)
    stat[0] = jnp.where(lanes == 0, top, jnp.where(lanes == 1, total, 0.0)).T[0:8]
    stats = [group(stat_p)]
    for n, step in enumerate(plane):
        send(stats[0], stat.at[0], stat_p.at[n], plane_to(*step))
    local_b = local.astype(BF16)

    def place(target, a, ky, kl, values):
        for hh in range(XH):
            block = values[hh * ZR : hh * ZR + ZR].reshape(Z, 8, values.shape[1]).astype(BF16)
            if a == 0:
                target[0, ky, hh * XL + kl] = block
            else:
                target[1, hh * XL + kl, ky] = block

    for ky in range(Y):
        values = rows_dot(local_b, tok[:, ky * XL * W : (ky + 1) * XL * W])
        for kl in range(XL):
            place(pb, 0, ky, kl, values[:, kl * W : (kl + 1) * W])
    moves = spread(pb, rb1, 0)

    arrive(line_move)
    got = line_rec[0]
    got = jnp.concatenate([got[:, T:], got[:, :T]], axis=1)
    high = jnp.maximum(slots_b, got[0:1])
    low = jnp.exp(slots_b - high)
    share = low / (sums_b * low + got[1:2] * jnp.exp(got[0:1] - high))
    comb = raised * share
    weight[...] = comb
    comb_b = comb.astype(BF16)
    for k in range(Y):
        values = rows_dot(comb_b, og[:, 2 * k * W : 2 * (k + 1) * W])
        for e in range(2):
            place(pb, 1, (2 * k + e) % Y, (2 * k + e) // Y, values[:, e * W : (e + 1) * W])
    moves.update(spread(pb, rb1, 1))
    sum_chunk, grad_chunk = end_of(reduce(pb, pb2, pb3, rb1, rb2, rbz, moves, stats))

    sum_chunk = sum_chunk / scale_in[pl.ds(own_row, 8), Z + 1 : Z + 2]
    seq_in[q, 0] = sum_chunk.astype(BF16)
    seq_in[q, 1] = grad_chunk.astype(BF16)
    before = len(groups) - 1
    seq_move = group(seq_in.at[0 : NQ - 1])
    for step in seq_far_first:
        send(seq_move, seq_in.at[q], seq_in.at[q], seq_to(*step)[1])
    sent(before)
    big[2].wait()
    big[3].wait()
    upper = lax.broadcasted_iota(jnp.int32, (8, 1), 0) < 4

    def pick(f, g):
        return jnp.where(upper, f, g)

    pre = hid_grad = None
    for step in ((0, 0),) + seq_far_first:
        if step == seq_far_first[0]:
            arrive(seq_move)
        k = seq_from(*step)
        slot_b, grad_b = (seq_in[k, a].astype(F32).astype(BF16) for a in range(2))
        more = [rows_dot(slot_b, win[e, columns(k, W), :]) for e in range(2)]
        pre = more if pre is None else [f + g for f, g in zip(pre, more)]
        more = [cols_dot(grad_b, wout[e, :, columns(by_x(k), W)]) for e in range(2)]
        hid_grad = more if hid_grad is None else [f + g for f, g in zip(hid_grad, more)]
    hidden, slope = gelu_and_slope(pick(*pre))
    hidden = hidden.astype(BF16)
    act = (pick(*hid_grad) * slope).astype(BF16)

    def products(step):
        k, device = seq_to(*step)
        in_part = pick(*(cols_dot(act, win[e, columns(k, W), :]) for e in range(2)))
        out_part = pick(*(rows_dot(hidden, wout[e, :, columns(by_x(k), W)]) for e in range(2)))
        return k, device, in_part.astype(BF16), out_part.astype(BF16)

    seq_move = group(seq_rec)
    order = seq_far_first + ((0, 0),)
    ready = products(order[0])
    for n, step in enumerate(order):
        k, device, in_part, out_part = ready
        if n + 1 < len(order):
            ready = products(order[n + 1])
        seq_out[k, 0] = in_part
        seq_out[k, 1] = out_part
        if step != (0, 0):
            send(seq_move, seq_out.at[k], seq_rec.at[step[0] * XL + step[1] - 1], device)
    arrive(seq_move)
    for a in (1, 0):
        total = seq_out[q, a].astype(F32)
        for i in range(NQ - 1):
            total += seq_rec[i, a].astype(F32)
        own_d[a] = total.astype(BF16)
    part = jnp.sum(sum_chunk * total.astype(BF16).astype(F32), axis=1, keepdims=True)
    spots = lax.broadcasted_iota(jnp.int32, (8, S), 1)
    cen[0] = jnp.where(spots == own_row + lines, part, 0.0)
    steps = gather(own_d, gath_d, (cen, cen_z, cen_p))
    next(steps)
    sent(seq_move + 1)
    *_, last = steps

    comb_g[...] = jnp.zeros_like(comb_g)
    disp_g[...] = jnp.zeros_like(disp_g)

    def back_disp(ky):
        span = columns(ky, XL * W)
        block = jnp.concatenate([flat(gath_d[0, ky, kl]) for kl in range(XL)], axis=1).astype(BF16)
        pair[0:S, span] = block
        disp_g[...] += rows_dot(block, tok_t[span, :])

    def back_comb(kx):
        kh, kl = div(kx, XL), rem(kx, XL)
        block = jnp.concatenate([flat(gath_d[1, ky, kl, kh]) for ky in range(Y)], axis=1).astype(BF16)
        comb_g[columns(kh, ZR), :] += rows_dot(block, og_t[columns(kl, Y * W), :])

    back_comb(x)
    back_disp(y)
    arrive(*last)
    for i in far_first:
        back_comb(rem(x + N - i, N))
    comb = weight[...]
    comb_grad = comb_g[...]
    mean = jnp.sum(comb * comb_grad, axis=0, keepdims=True)
    line[1] = jnp.broadcast_to(mean, (8, 2 * T))
    line_move = group(line_rec.at[1])
    send(line_move, line.at[1], line_rec.at[1], other)
    for i in far_first:
        back_disp(rem(y + N - i, N))
    centre_row = cen[1]
    for n in range(N * N - 1):
        centre_row += cen_p[n]
    centre = jnp.broadcast_to(jnp.sum(centre_row, axis=0, keepdims=True), (128, S)).T[:, 0:1]
    disp = jnp.exp(logits[...] - scale_out[:, Z : Z + 1]) / scale_out[:, Z + 1 : Z + 2]
    disp_part = disp * (disp_g[...] - centre)
    arrive(line_move)
    got = line_rec[1]
    mean = mean + jnp.concatenate([got[:, T:], got[:, :T]], axis=1)[0:1]
    logit_grad = disp_part + comb * (comb_grad - mean)
    logit_b = logit_grad.astype(BF16)

    for ky in range(Y):
        values = rows_dot(logit_b, tok[:, ky * XL * W : (ky + 1) * XL * W])
        for kl in range(XL):
            for a in range(2):
                place(pg, a, ky, kl, values[:, (2 * kl + a) * HALF : (2 * kl + a + 1) * HALF])
    moves = {**spread(pg, rg1, 0), **spread(pg, rg1, 1)}
    both[:, 0:S] = disp.T.astype(BF16)
    both[:, S : 2 * S] = logit_grad.T.astype(BF16)

    def their_grads(k, _):
        tg_send[:, columns(k, W)] = rows_dot(both[T : 2 * T], pair[:, columns(k, W)]).astype(BF16)
        return 0

    lax.fori_loop(0, NQ, their_grads, 0)
    tg_move = group(tg_rec)
    send(tg_move, tg_send, tg_rec, other)
    steps = reduce(pg, pg2, pg3, rg1, rg2, rgz, moves)
    next(steps)
    arrive(tg_move)

    def own_grads(k, _):
        span = columns(k, W)
        tg[:, span] = (rows_dot(both[0:T], pair[:, span]) + tg_rec[:, span].astype(F32)).astype(BF16)
        return 0

    lax.fori_loop(0, NQ, own_grads, 0)
    next(steps)
    sent(len(groups) - 1)
    parts = end_of(steps)
    for a in range(2):
        sg_out[:, a * HALF : (a + 1) * HALF] = parts[a]
    sent(len(groups))
    assert len(groups) == send_sem.shape[0], len(groups)


def shards(sizes, tokens, slot_embed, expert_in, expert_out, out_grad):
    Y, XL, Z, XH, C = sizes
    N, NQ = XL * XH, Y * XL
    T, D = tokens.shape
    S = slot_embed.shape[1] * Z * XH
    W = D // NQ
    H = W // 2
    vm = pltpu.VMEM

    def reduce_buffers(w):
        return [
            vm((2, N, N, Z, 8, w), BF16),
            vm((2, N, Z, 8, w), BF16),
            vm((2, Z, 8, w), BF16),
            vm((2, N - 1, N, Z, 8, w), BF16),
            vm((2, N - 1, Z, 8, w), BF16),
            vm((Z, 2, 8, w), BF16),
        ]

    n = 42
    scratch = [
        vm((2 * T, D), BF16), vm((2 * T, D), BF16), vm(expert_in.shape, BF16), vm(expert_out.shape, BF16),
        vm((D, 2 * T), BF16), vm((D, 2 * T), BF16), vm((2 * S, D), BF16),
        vm((S, 2 * T), F32), vm((S, 2 * T), F32), vm((S, 2 * T), F32), vm((S, 2 * T), F32),
        vm((2 * T, 2 * S), BF16), vm((T, D), BF16), vm((T, D), BF16),
        vm((2, 8, H), BF16), vm((2, 8, W), BF16), vm((2, Y, XL, XH, Z, 8, H), BF16), vm((2, Y, XL, XH, Z, 8, W), BF16),
        *reduce_buffers(W), *reduce_buffers(H),
        vm((2, 8, S), F32), vm((N * N - 1, 8, S), F32), vm((Z - 1, 8, S), F32),
        vm((2, S, 128), F32), vm((S, 128), F32), vm((S, 128), F32),
        vm((2, 8, S), F32), vm((Z, 8, S), F32), vm((N * N - 1, 8, S), F32),
        vm((NQ, 2, 8, W), BF16), vm((NQ, 2, 8, W), BF16), vm((NQ - 1, 2, 8, W), BF16),
        vm((2, 8, 2 * T), F32), vm((2, 8, 2 * T), F32),
        pltpu.SemaphoreType.DMA((6,)), pltpu.SemaphoreType.DMA((n,)), pltpu.SemaphoreType.DMA((n,)),
    ]
    hbm = pl.BlockSpec(memory_space=pl.ANY)
    tok_grad, slot_grad = pl.pallas_call(
        functools.partial(kernel, sizes),
        out_shape=(pltpu.VMEM((T, D), BF16), pltpu.VMEM((8, W), F32)),
        in_specs=[hbm] * 5,
        out_specs=(pl.BlockSpec(memory_space=pltpu.VMEM), pl.BlockSpec(memory_space=pltpu.VMEM)),
        scratch_shapes=scratch,
        compiler_params=pltpu.CompilerParams(collective_id=0, has_side_effects=True),
        name="soft_moe",
    )(tokens, slot_embed.T, expert_in, expert_out, out_grad)
    return tok_grad, slot_grad.T


SIZES = (4, 2, 8, 2, 2)


def solution(mesh, sizes=SIZES):
    torus = Mesh(mesh.devices.reshape(sizes), AXES)
    placed = (
        P(SEQ_EXP, None),
        P(None, EXP),
        P(EXP, None, SEQ),
        P(EXP, SEQ, None),
        P(SEQ_EXP, None),
    )
    return jax.shard_map(
        functools.partial(shards, sizes),
        mesh=torus,
        in_specs=placed,
        out_specs=(P(SEQ_EXP, None), P(SEQ, EXP)),
        check_vma=False,
    )
```

time: 90.1 us -> 81.9 us (0.909)
  Pallas kernels: 87.8 us -> 79.6 us
    pallas_call x1, Pallas kernels: 87.8 us -> 79.6 us  [shards(): pl.pallas_call(functools.partial(kernel, sizes), out_shape=(pltpu.VMEM((T...]
where the time goes in v3:
time: 81.9 us; the launch traced here: 81.8 us
  Pallas kernels  79.6 us (97%)
  local copies, waits for them, and re-layouts  1.57 us (2%)
    pallas_call x1, Pallas kernels, shards(): pl.pallas_call(functools.partial(kernel, sizes), out_shape=(pltpu.VMEM((T...  79.6 us

profile of v3, /device:TPU:1, one launch (start us, length us, event | category | flops | bytes accessed | tf_op | source)
XLA Modules:
  0.0 81.8 jit_solution(5954537963334714201)
XLA Ops:
  0.6 79.6 %soft_moe.1 = (bf16[256,2048]{1,0:T(8,128)(2,1)S(1)}, f32[8,256]{1,0:T(8,128)S(1)}) custom-call(bf16[256,2048]{1,0:T(8,128)(2,1)} %tok_hbm.1, bf16[8,2048]{1,0:T(8,128)(2,1)} %bitcast.3, bf16[2,2048,512]{2,1,0:T(8,128)(2,1)} %win_hbm.1, bf16[2,512,2048]{2,1,0:T(8,128)(2,1)} %wout_hbm.1, bf16[256,2048]{1,0:T(8,128)(2,1)} %og_hbm.1), custom_call_target="tpu_custom_call" | custom-call | tf_op jit(solution)/shard_map/soft_moe/pallas_call | solution.py:552
  80.2 1.0 %copy.9 = bf16[256,2048]{1,0:T(8,128)(2,1)} copy(bf16[256,2048]{1,0:T(8,128)(2,1)S(1)} %get-tuple-element.6) | data formatting | bytes 2097152
  81.2 0.6 copy.10

commit v4 on v3

--- a/solution.py
+++ b/solution.py
@@ -41,12 +41,13 @@
     tok_hbm, slot_hbm, win_hbm, wout_hbm, og_hbm,
     tg, sg_out,
     tok, og, win, wout, tok_t, og_t, pair, logits, weight, comb_g, disp_g, both, tg_send, tg_rec,
-    own_a, own_d, gath_a, gath_d,
-    pb, pb2, pb3, rb1, rb2, rbz,
+    own_a, own_s, own_g, gath_a, gath_s, gath_g,
+    ps, ps2, ps3, rs1, rs2, rsz,
+    pw, pw2, pw3, rw1, rw2, rwz,
     pg, pg2, pg3, rg1, rg2, rgz,
     stat, stat_p, stat_z, factor, scale_out, scale_in,
     cen, cen_z, cen_p,
-    seq_in, seq_out, seq_rec, line, line_rec,
+    in_s, in_g, out_s, out_g, rec_s, rec_g, line, line_rec,
     local_sem, send_sem, recv_sem,
 ):
     Y, XL, Z, XH, C = sizes
@@ -88,9 +89,6 @@
     def seq_from(dy, dl):
         return rem(y + N - dy, N) * XL + rem(xl + dl, XL)
 
-    def by_x(k):
-        return rem(k, XL) * Y + div(k, XL)
-
     other = {"exp_2": 1 - c}
     far_first = (2, 1, 3)
     z_far_first = sorted(range(Z), key=lambda i: -min(i, Z - i))
@@ -128,7 +126,7 @@
             own_a.at[a],
             local_sem.at[a],
         )
-        for a, start in ((0, y * XL + xl), (1, NQ + xl * Y + y))
+        for a, start in ((0, xl * Y + y), (1, NQ + y * XL + xl))
     ]
     big = [
         pltpu.make_async_copy(src, dst, local_sem.at[2 + k])
@@ -165,16 +163,17 @@
             hops[i] = group(buf.at[:, y, xl, xh])
             send(hops[i], buf.at[0, y, xl, xh], buf.at[0, y, xl, xh], x_to(i)[1])
             send(hops[i], buf.at[1, y, xl, xh], buf.at[1, y, xl, xh], y_to(i)[1])
-        last = [group(buf.at[:, 0 : N - 1])]
+        last = {}
 
         def pass_on(j):
+            last[j] = group(buf.at[:, 0 : N - 1, 0, 0])
             kx = rem(x + N - j, N)
             part = buf.at[0, y, rem(kx, XL), div(kx, XL)]
             for i in far_first:
-                send(last[0], part, part, y_to(i)[1])
+                send(last[j], part, part, y_to(i)[1])
             part = buf.at[1, rem(y + N - j, N), xl, xh]
             for i in far_first:
-                send(last[0], part, part, x_to(i)[1])
+                send(last[j], part, part, x_to(i)[1])
 
         pass_on(0)
         if beside:
@@ -182,9 +181,9 @@
             for i in range(1, Z):
                 total += over_z[i]
             own[1] = total
-            last.append(group(over_plane))
+            last["rows"] = group(over_plane)
             for n, step in enumerate(plane):
-                send(last[1], own.at[1], over_plane.at[n], plane_to(*step))
+                send(last["rows"], own.at[1], over_plane.at[n], plane_to(*step))
         yield
         for j in (1, 3, 2):
             arrive(hops[j])
@@ -224,24 +223,28 @@
         scaled = stats is not None
         if scaled:
             arrive(*stats)
+            halves = lambda e: (e[:, 0:S], e[:, S : 2 * S])
             stat_of = {(0, 0): stat[0]}
             for n, step in enumerate(plane):
                 stat_of[step] = stat_p[n]
-            by_y = [merge([(e[0:1], e[1:2]) for e in (stat_of[i, j] for i in range(N))]) for j in range(N)]
-            merged, across = merge([joint for joint, _ in by_y])
-            stat[1] = jnp.where(lines == 0, merged[0], merged[1])
+            by_y = [merge([halves(stat_of[i, j]) for i in range(N)]) for j in range(N)]
+            by_x = [merge([halves(stat_of[i, j]) for j in range(N)]) for i in range(N)]
+            merged, across_x = merge([joint for joint, _ in by_y])
+            _, across_y = merge([joint for joint, _ in by_x])
+            stat[1] = jnp.concatenate(merged, axis=1)
             stats = [group(stat_z)]
             for i in z_far_first:
                 if i:
                     send(stats[0], stat.at[1], stat_z.at[i - 1], z_to(i)[1])
-            factor[0] = upright(by_y[0][1])
-            factor[1] = upright(across)
+            for k, rows in enumerate((by_y[0][1], by_x[0][1], across_x, across_y)):
+                factor[k] = upright(rows)
         later = [group(r2)]
         for j in far_first + (0,):
             for a, me, (b, device) in ((0, y, x_to(j)), (1, x, y_to(j))):
                 arrive(moves[a, j])
                 parts = [p[a, me, b]] + [r1[a, i, b] for i in range(N - 1)]
-                total = joined(parts, factor.at[0] if scaled and a == 0 else None, div(b, XL) * ZR, ZR)
+                row = (div(b, XL) if a == 0 else xh) * ZR
+                total = joined(parts, factor.at[a] if scaled else None, row, ZR)
                 s2[a, b] = total.reshape(Z, 8, w).astype(BF16)
                 if j:
                     send(later[0], s2.at[a, b], r2.at[a, j - 1], device)
@@ -250,14 +253,14 @@
         if scaled:
             arrive(*stats)
             entries = [stat[1]] + [stat_z[i] for i in range(Z - 1)]
-            merged, across = merge([(e[0:1], e[1:2]) for e in entries])
+            merged, across = merge([halves(e) for e in entries])
             scale_out[...] = upright(across + list(merged))
             scale_move = group(scale_in)
             send(scale_move, scale_out, scale_in, other)
         arrive(*moves)
         for a, me in ((0, x), (1, y)):
             parts = [s2[a, me]] + [r2[a, i] for i in range(N - 1)]
-            total = joined(parts, factor.at[1] if scaled and a == 0 else None, xh * ZR, ZR)
+            total = joined(parts, factor.at[2 + a] if scaled else None, xh * ZR, ZR)
             s3[a] = total.reshape(Z, 8, w).astype(BF16)
         moves = [group(rz)]
         for i in z_far_first:
@@ -270,7 +273,7 @@
         result = []
         for a in range(2):
             parts = [rz[i, a] for i in range(Z)]
-            result.append(joined(parts, scale_in if scaled and a == 0 else None, own_row, 8))
+            result.append(joined(parts, scale_in if scaled else None, own_row, 8))
         yield result
 
     def spread(p, r1, a):
@@ -308,29 +311,25 @@
     last = next(steps)
     logits[...] = jnp.zeros_like(logits)
 
-    def table_by_y(ky):
-        span = columns(ky, XL * HALF)
-        block = jnp.concatenate([flat(gath_a[0, ky, kl]) for kl in range(XL)], axis=1).astype(BF16)
+    def use_table(j):
+        ky, kx = rem(y + N - j, N), rem(x + N - j, N)
+        kh, kl = div(kx, XL), rem(kx, XL)
+        span = columns(kl, Y * HALF)
+        block = jnp.concatenate([flat(gath_a[0, k, kl, kh]) for k in range(Y)], axis=1).astype(BF16)
+        pair[pl.ds(pl.multiple_of(S + kh * ZR, ZR), ZR), span] = block
+        logits[columns(kh, ZR), :] += rows_dot(block, tok_t[span, :])
+        span = pl.ds(pl.multiple_of(NQ * HALF + ky * (XL * HALF), HALF), XL * HALF)
+        block = jnp.concatenate([flat(gath_a[1, ky, k]) for k in range(XL)], axis=1).astype(BF16)
         pair[S : 2 * S, span] = block
         logits[...] += rows_dot(block, tok_t[span, :])
-
-    def table_by_x(kx):
-        kh, kl = div(kx, XL), rem(kx, XL)
-        span = pl.ds(pl.multiple_of(NQ * HALF + kl * (Y * HALF), HALF), Y * HALF)
-        block = jnp.concatenate([flat(gath_a[1, ky, kl, kh]) for ky in range(Y)], axis=1).astype(BF16)
-        pair[pl.ds(pl.multiple_of(S + kh * ZR, ZR), ZR), span] = block
-        logits[columns(kh, ZR), :] += rows_dot(block, tok_t[span, :])
 
     big[1].wait()
     turn(og, og_t, 0)
     arrive(swaps[1])
     turn(og, og_t, 1)
-    table_by_y(y)
-    table_by_x(x)
-    arrive(*last)
-    for i in far_first:
-        table_by_y(rem(y + N - i, N))
-        table_by_x(rem(x + N - i, N))
+    for j in (0, 1, 3, 2):
+        arrive(last[j])
+        use_table(j)
     lg = logits[...]
 
     slots_b = jnp.max(lg, axis=0, keepdims=True)
@@ -344,7 +343,8 @@
     local = jnp.exp(lg - top)
     total = jnp.sum(local, axis=1, keepdims=True)
     lanes = lax.broadcasted_iota(jnp.int32, (S, 128), 1)
-    stat[0] = jnp.where(lanes == 0, top, jnp.where(lanes == 1, total, 0.0)).T[0:8]
+    turned = jnp.where(lanes == 0, top, jnp.where(lanes == 1, total, 0.0)).T
+    stat[0] = jnp.concatenate([turned[0:1], turned[1:2]], axis=1)
     stats = [group(stat_p)]
     for n, step in enumerate(plane):
         send(stats[0], stat.at[0], stat_p.at[n], plane_to(*step))
@@ -358,11 +358,15 @@
             else:
                 target[1, hh * XL + kl, ky] = block
 
-    for ky in range(Y):
-        values = rows_dot(local_b, tok[:, ky * XL * W : (ky + 1) * XL * W])
-        for kl in range(XL):
-            place(pb, 0, ky, kl, values[:, kl * W : (kl + 1) * W])
-    moves = spread(pb, rb1, 0)
+    def partial_sums(rows, patches, p, r1):
+        for ky in range(Y):
+            values = rows_dot(rows, patches[:, ky * XL * W : (ky + 1) * XL * W])
+            for kl in range(XL):
+                for a in range(2):
+                    place(p, a, ky, kl, values[:, (2 * kl + a) * HALF : (2 * kl + a + 1) * HALF])
+        return {**spread(p, r1, 0), **spread(p, r1, 1)}
+
+    slot_moves = partial_sums(local_b, tok, ps, rs1)
 
     arrive(line_move)
     got = line_rec[0]
@@ -373,104 +377,130 @@
     comb = raised * share
     weight[...] = comb
     comb_b = comb.astype(BF16)
-    for k in range(Y):
-        values = rows_dot(comb_b, og[:, 2 * k * W : 2 * (k + 1) * W])
-        for e in range(2):
-            place(pb, 1, (2 * k + e) % Y, (2 * k + e) // Y, values[:, e * W : (e + 1) * W])
-    moves.update(spread(pb, rb1, 1))
-    sum_chunk, grad_chunk = end_of(reduce(pb, pb2, pb3, rb1, rb2, rbz, moves, stats))
-
-    sum_chunk = sum_chunk / scale_in[pl.ds(own_row, 8), Z + 1 : Z + 2]
-    seq_in[q, 0] = sum_chunk.astype(BF16)
-    seq_in[q, 1] = grad_chunk.astype(BF16)
-    before = len(groups) - 1
-    seq_move = group(seq_in.at[0 : NQ - 1])
-    for step in seq_far_first:
-        send(seq_move, seq_in.at[q], seq_in.at[q], seq_to(*step)[1])
+    grad_moves = partial_sums(comb_b, og, pw, rw1)
+
+    slot_steps = reduce(ps, ps2, ps3, rs1, rs2, rsz, slot_moves, stats)
+    grad_steps = reduce(pw, pw2, pw3, rw1, rw2, rwz, grad_moves)
+    next(slot_steps)
+    next(grad_steps)
+    next(slot_steps)
+    next(grad_steps)
+    before = len(groups) - 2
+    upper = lax.broadcasted_iota(jnp.int32, (8, 1), 0) < 4
+    seq_rings = (((2, 1),), ((2, 0), (1, 1), (3, 1)), ((1, 0), (3, 0), (0, 1)))
+    order = seq_far_first + ((0, 0),)
+
+    def pick(f, g):
+        return jnp.where(upper, f, g)
+
+    def seq_send(buf):
+        moves = {}
+        for ring in seq_rings:
+            moves[ring[0]] = group(buf.at[0 : len(ring)])
+            for step in ring:
+                send(moves[ring[0]], buf.at[q], buf.at[q], seq_to(*step)[1])
+        return moves
+
+    def seq_use(buf, moves, product):
+        total = None
+        for step in ((0, 0),) + sum(seq_rings[::-1], ()):
+            if step in moves:
+                arrive(moves[step])
+            k = seq_from(*step)
+            rows = buf[k].astype(F32).astype(BF16)
+            more = [product(rows, e, columns(k, W)) for e in range(2)]
+            total = more if total is None else [f + g for f, g in zip(total, more)]
+        return pick(*total)
+
+    def seq_give(buf, rec, product):
+        move = group(rec)
+        ready = product(columns(seq_to(*order[0])[0], W))
+        for n, step in enumerate(order):
+            now = ready
+            if n + 1 < len(order):
+                ready = product(columns(seq_to(*order[n + 1])[0], W))
+            k, device = seq_to(*step)
+            buf[k] = now.astype(BF16)
+            if step != (0, 0):
+                send(move, buf.at[k], rec.at[step[0] * XL + step[1] - 1], device)
+        return move
+
+    def seq_sum(buf, rec, target):
+        total = buf[q].astype(F32)
+        for i in range(NQ - 1):
+            total += rec[i].astype(F32)
+        total = total.astype(BF16)
+        for a in range(2):
+            target[a] = total[:, a * HALF : (a + 1) * HALF]
+        return total.astype(F32)
+
+    sum_chunk = jnp.concatenate(next(slot_steps), axis=1) / scale_in[pl.ds(own_row, 8), Z + 1 : Z + 2]
+    in_s[q] = sum_chunk.astype(BF16)
+    slot_moves = seq_send(in_s)
+    in_g[q] = jnp.concatenate(next(grad_steps), axis=1).astype(BF16)
+    grad_moves = seq_send(in_g)
     sent(before)
     big[2].wait()
     big[3].wait()
-    upper = lax.broadcasted_iota(jnp.int32, (8, 1), 0) < 4
-
-    def pick(f, g):
-        return jnp.where(upper, f, g)
-
-    pre = hid_grad = None
-    for step in ((0, 0),) + seq_far_first:
-        if step == seq_far_first[0]:
-            arrive(seq_move)
-        k = seq_from(*step)
-        slot_b, grad_b = (seq_in[k, a].astype(F32).astype(BF16) for a in range(2))
-        more = [rows_dot(slot_b, win[e, columns(k, W), :]) for e in range(2)]
-        pre = more if pre is None else [f + g for f, g in zip(pre, more)]
-        more = [cols_dot(grad_b, wout[e, :, columns(by_x(k), W)]) for e in range(2)]
-        hid_grad = more if hid_grad is None else [f + g for f, g in zip(hid_grad, more)]
-    hidden, slope = gelu_and_slope(pick(*pre))
+    pre = seq_use(in_s, slot_moves, lambda rows, e, span: rows_dot(rows, win[e, span, :]))
+    hidden, slope = gelu_and_slope(pre)
     hidden = hidden.astype(BF16)
-    act = (pick(*hid_grad) * slope).astype(BF16)
-
-    def products(step):
-        k, device = seq_to(*step)
-        in_part = pick(*(cols_dot(act, win[e, columns(k, W), :]) for e in range(2)))
-        out_part = pick(*(rows_dot(hidden, wout[e, :, columns(by_x(k), W)]) for e in range(2)))
-        return k, device, in_part.astype(BF16), out_part.astype(BF16)
-
-    seq_move = group(seq_rec)
-    order = seq_far_first + ((0, 0),)
-    ready = products(order[0])
-    for n, step in enumerate(order):
-        k, device, in_part, out_part = ready
-        if n + 1 < len(order):
-            ready = products(order[n + 1])
-        seq_out[k, 0] = in_part
-        seq_out[k, 1] = out_part
-        if step != (0, 0):
-            send(seq_move, seq_out.at[k], seq_rec.at[step[0] * XL + step[1] - 1], device)
-    arrive(seq_move)
-    for a in (1, 0):
-        total = seq_out[q, a].astype(F32)
-        for i in range(NQ - 1):
-            total += seq_rec[i, a].astype(F32)
-        own_d[a] = total.astype(BF16)
-    part = jnp.sum(sum_chunk * total.astype(BF16).astype(F32), axis=1, keepdims=True)
+    slot_move = seq_give(out_s, rec_s, lambda span: pick(*(rows_dot(hidden, wout[e, :, span]) for e in range(2))))
+    hid_grad = seq_use(in_g, grad_moves, lambda rows, e, span: cols_dot(rows, wout[e, :, span]))
+    act = (hid_grad * slope).astype(BF16)
+    grad_move = seq_give(out_g, rec_g, lambda span: pick(*(cols_dot(act, win[e, span, :]) for e in range(2))))
+    arrive(slot_move)
+    seq_sum(out_s, rec_s, own_s)
+    slot_steps = gather(own_s, gath_s)
+    next(slot_steps)
+    arrive(grad_move)
+    total = seq_sum(out_g, rec_g, own_g)
+    part = jnp.sum(sum_chunk * total, axis=1, keepdims=True)
     spots = lax.broadcasted_iota(jnp.int32, (8, S), 1)
-    cen[0] = jnp.where(spots == own_row + lines, part, 0.0)
-    steps = gather(own_d, gath_d, (cen, cen_z, cen_p))
-    next(steps)
-    sent(seq_move + 1)
-    *_, last = steps
+    cen[0] = jnp.sum(jnp.where(spots == own_row + lines, part, 0.0), axis=0, keepdims=True)
+    grad_steps = gather(own_g, gath_g, (cen, cen_z, cen_p))
+    next(grad_steps)
+    sent(grad_move + 1)
+    next(slot_steps)
+    next(grad_steps)
+    slot_last = next(slot_steps)
+    grad_last = next(grad_steps)
 
     comb_g[...] = jnp.zeros_like(comb_g)
     disp_g[...] = jnp.zeros_like(disp_g)
 
-    def back_disp(ky):
-        span = columns(ky, XL * W)
-        block = jnp.concatenate([flat(gath_d[0, ky, kl]) for kl in range(XL)], axis=1).astype(BF16)
-        pair[0:S, span] = block
-        disp_g[...] += rows_dot(block, tok_t[span, :])
-
-    def back_comb(kx):
+    def back(j, buf, right, target, keep):
+        ky, kx = rem(y + N - j, N), rem(x + N - j, N)
         kh, kl = div(kx, XL), rem(kx, XL)
-        block = jnp.concatenate([flat(gath_d[1, ky, kl, kh]) for ky in range(Y)], axis=1).astype(BF16)
-        comb_g[columns(kh, ZR), :] += rows_dot(block, og_t[columns(kl, Y * W), :])
-
-    back_comb(x)
-    back_disp(y)
-    arrive(*last)
-    for i in far_first:
-        back_comb(rem(x + N - i, N))
+        for a, rows, spots in (
+            (0, columns(kh, ZR), [(k, kl) for k in range(Y)]),
+            (1, pl.ds(0, S), [(ky, k) for k in range(XL)]),
+        ):
+            spans = [pl.ds(pl.multiple_of((f * XL + g) * W + a * HALF, HALF), HALF) for f, g in spots]
+            blocks = [flat(buf[0, f, g, kh] if a == 0 else buf[1, f, g]) for f, g in spots]
+            if keep:
+                for span, block in zip(spans, blocks):
+                    pair[rows, span] = block.astype(BF16)
+            block = jnp.concatenate(blocks, axis=1).astype(BF16)
+            target[rows, :] += rows_dot(block, jnp.concatenate([right[span, :] for span in spans], axis=0))
+
+    for j in (0, 1, 3, 2):
+        arrive(slot_last[j])
+        back(j, gath_s, og_t, comb_g, False)
     comb = weight[...]
     comb_grad = comb_g[...]
     mean = jnp.sum(comb * comb_grad, axis=0, keepdims=True)
     line[1] = jnp.broadcast_to(mean, (8, 2 * T))
     line_move = group(line_rec.at[1])
     send(line_move, line.at[1], line_rec.at[1], other)
-    for i in far_first:
-        back_disp(rem(y + N - i, N))
+    for j in (0, 1, 3, 2):
+        arrive(grad_last[j])
+        back(j, gath_g, tok_t, disp_g, True)
+    arrive(grad_last["rows"])
     centre_row = cen[1]
     for n in range(N * N - 1):
         centre_row += cen_p[n]
-    centre = jnp.broadcast_to(jnp.sum(centre_row, axis=0, keepdims=True), (128, S)).T[:, 0:1]
+    centre = jnp.broadcast_to(centre_row, (128, S)).T[:, 0:1]
     disp = jnp.exp(logits[...] - scale_out[:, Z : Z + 1]) / scale_out[:, Z + 1 : Z + 2]
     disp_part = disp * (disp_g[...] - centre)
     arrive(line_move)
@@ -479,12 +509,7 @@
     logit_grad = disp_part + comb * (comb_grad - mean)
     logit_b = logit_grad.astype(BF16)
 
-    for ky in range(Y):
-        values = rows_dot(logit_b, tok[:, ky * XL * W : (ky + 1) * XL * W])
-        for kl in range(XL):
-            for a in range(2):
-                place(pg, a, ky, kl, values[:, (2 * kl + a) * HALF : (2 * kl + a + 1) * HALF])
-    moves = {**spread(pg, rg1, 0), **spread(pg, rg1, 1)}
+    moves = partial_sums(logit_b, tok, pg, rg1)
     both[:, 0:S] = disp.T.astype(BF16)
     both[:, S : 2 * S] = logit_grad.T.astype(BF16)
 
@@ -533,18 +558,18 @@
             vm((Z, 2, 8, w), BF16),
         ]
 
-    n = 42
+    n = 72
     scratch = [
         vm((2 * T, D), BF16), vm((2 * T, D), BF16), vm(expert_in.shape, BF16), vm(expert_out.shape, BF16),
         vm((D, 2 * T), BF16), vm((D, 2 * T), BF16), vm((2 * S, D), BF16),
         vm((S, 2 * T), F32), vm((S, 2 * T), F32), vm((S, 2 * T), F32), vm((S, 2 * T), F32),
         vm((2 * T, 2 * S), BF16), vm((T, D), BF16), vm((T, D), BF16),
-        vm((2, 8, H), BF16), vm((2, 8, W), BF16), vm((2, Y, XL, XH, Z, 8, H), BF16), vm((2, Y, XL, XH, Z, 8, W), BF16),
-        *reduce_buffers(W), *reduce_buffers(H),
-        vm((2, 8, S), F32), vm((N * N - 1, 8, S), F32), vm((Z - 1, 8, S), F32),
-        vm((2, S, 128), F32), vm((S, 128), F32), vm((S, 128), F32),
-        vm((2, 8, S), F32), vm((Z, 8, S), F32), vm((N * N - 1, 8, S), F32),
-        vm((NQ, 2, 8, W), BF16), vm((NQ, 2, 8, W), BF16), vm((NQ - 1, 2, 8, W), BF16),
+        *[vm((2, 8, H), BF16)] * 3, *[vm((2, Y, XL, XH, Z, 8, H), BF16)] * 3,
+        *reduce_buffers(H), *reduce_buffers(H), *reduce_buffers(H),
+        vm((2, 1, 2 * S), F32), vm((N * N - 1, 1, 2 * S), F32), vm((Z - 1, 1, 2 * S), F32),
+        vm((4, S, 128), F32), vm((S, 128), F32), vm((S, 128), F32),
+        vm((2, 1, S), F32), vm((Z, 1, S), F32), vm((N * N - 1, 1, S), F32),
+        *[vm((NQ, 8, W), BF16)] * 4, *[vm((NQ - 1, 8, W), BF16)] * 2,
         vm((2, 8, 2 * T), F32), vm((2, 8, 2 * T), F32),
         pltpu.SemaphoreType.DMA((6,)), pltpu.SemaphoreType.DMA((n,)), pltpu.SemaphoreType.DMA((n,)),
     ]

time: 81.9 us -> 75.8 us (0.926)
  Pallas kernels: 79.6 us -> 73.5 us
    pallas_call x1, Pallas kernels: 79.6 us -> 73.5 us  [shards(): pl.pallas_call(functools.partial(kernel, sizes), out_shape=(pltpu.VMEM((T...]
where the time goes in v4:
time: 75.8 us; the launch traced here: 75.7 us
  Pallas kernels  73.5 us (97%)
  local copies, waits for them, and re-layouts  1.57 us (2%)
    pallas_call x1, Pallas kernels, shards(): pl.pallas_call(functools.partial(kernel, sizes), out_shape=(pltpu.VMEM((T...  73.5 us
    unnamed x2, local copies, waits for them, and re-layouts  1.57 us

profile of v4, /device:TPU:1, one launch (start us, length us, event | category | flops | bytes accessed | tf_op | source)
XLA Modules:
  0.0 75.7 jit_solution(15938710946198492687)
XLA Ops:
  0.6 73.5 %soft_moe.1 = (bf16[256,2048]{1,0:T(8,128)(2,1)S(1)}, f32[8,256]{1,0:T(8,128)S(1)}) custom-call(bf16[256,2048]{1,0:T(8,128)(2,1)} %tok_hbm.1, bf16[8,2048]{1,0:T(8,128)(2,1)} %bitcast.3, bf16[2,2048,512]{2,1,0:T(8,128)(2,1)} %win_hbm.1, bf16[2,512,2048]{2,1,0:T(8,128)(2,1)} %wout_hbm.1, bf16[256,2048]{1,0:T(8,128)(2,1)} %og_hbm.1), custom_call_target="tpu_custom_call" | custom-call | tf_op jit(solution)/shard_map/soft_moe/pallas_call | solution.py:577
  74.1 1.0 %copy.9 = bf16[256,2048]{1,0:T(8,128)(2,1)} copy(bf16[256,2048]{1,0:T(8,128)(2,1)S(1)} %get-tuple-element.6) | data formatting | bytes 2097152
  75.1 0.6 copy.10
